TPU v7x, 64 devices: a 2x2x8 block of a 4x4x8 slice. The times are simulated.
64 devices in a mesh: data: 4 (over x, y), sp: 16 (over z, core).
Axes of the slice: x: 2, y: 2, z: 8, core: 2. Of those that a mesh axis runs over, the one named last changes fastest.
The devices are a block of a 4x4x8 slice.
Arguments:
- latents: bfloat16 [8, 48, 256, 384], P('data', 'sp'), parts along dimension 0
- norms: float32 [4, 4, 384], replicated
- w_qkv: bfloat16 [4, 384, 3, 6, 64], replicated
- w_out: bfloat16 [4, 6, 64, 384], replicated
- w_up: bfloat16 [4, 384, 1536], replicated
- w_down: bfloat16 [4, 1536, 384], replicated
Outputs:
- output: bfloat16 [8, 48, 256, 384], P('data', None, 'sp'), parts along dimension 0
There are 4 independent parts. A program takes and returns all parts, laid end to end along the dimension named above; an argument that names none is the same for every part.
All inputs are finite; a program needn't handle non-finite values.
Results may differ from a plain program's by a relative error of at most 0.0161434.
Values are sent between devices in bfloat16 or wider.
A program may use at most 768 MiB of HBM per device.

v0:
```python
import functools
import math
import jax
import jax.numpy as jnp
from jax import lax
from jax.experimental import pallas as pl
from jax.experimental.pallas import tpu as pltpu
from jax.sharding import PartitionSpec as P

EPS = 1e-6
LANES = 128
MASKED = -1e38
F32, BF16 = jnp.float32, jnp.bfloat16


def dot(a, b):
    return jnp.dot(a, b, preferred_element_type=F32)


def dot_nt(a, b):
    return lax.dot_general(a, b, (((1,), (1,)), ((), ())), preferred_element_type=F32)


def layer_norm(x, gain, shift):
    centered = x - jnp.mean(x, axis=-1, keepdims=True)
    variance = jnp.mean(centered * centered, axis=-1, keepdims=True)
    return centered * lax.rsqrt(variance + EPS) * gain + shift


def kernel(n, head, x_ref, norms, wqkv_hbm, wout_hbm, wup_hbm, wdown_hbm, y_ref,
           wqkv, wout, wup, wdown, s_in, s_out, t_in, t_out, qkv_s, attn_s, hid_s, a_f32, o_f32, mask_s,
           w_sem, x_sem, b_recv, ac_recv, b_send, ac_send, y_sem):
    pairs, videos, f_loc, patches, width = s_in.shape
    frames, p_loc = t_in.shape[2], t_in.shape[3]
    rows_t = frames * p_loc
    me = lax.axis_index("sp")
    pair_heads = width // LANES
    group = 4
    rows_g = group * frames
    scale = head ** -0.5

    barrier = pltpu.get_barrier_semaphore()

    def tell(step, c):
        pl.semaphore_signal(barrier, inc=1, device_id={"sp": lax.rem(me + step, n)})
        return c

    lax.fori_loop(1, n, tell, 0)

    def weight_copies(layer):
        return [pltpu.make_async_copy(src.at[layer], dst.at[layer], w_sem.at[layer, i])
                for i, (src, dst) in enumerate(((wqkv_hbm, wqkv), (wout_hbm, wout), (wup_hbm, wup), (wdown_hbm, wdown)))]

    def start_weights(layer):
        for c in weight_copies(layer):
            c.start()

    for v in range(videos):
        pltpu.make_async_copy(x_ref.at[v], s_in.at[0, v], x_sem.at[v]).start()
    start_weights(0)

    row_p = lax.broadcasted_iota(jnp.int32, (rows_g, rows_g), 0)
    col_p = lax.broadcasted_iota(jnp.int32, (rows_g, rows_g), 1)
    same = jnp.zeros((rows_g, rows_g), F32)
    for i in range(group):
        lo, hi = i * frames, (i + 1) * frames
        inside = (row_p >= lo) & (row_p < hi) & (col_p >= lo) & (col_p < hi)
        same = jnp.where(inside, 1.0, same)
    mask_s[...] = same

    lane = lax.broadcasted_iota(jnp.int32, (1, LANES), 1)
    keep = [jnp.where(lane // head == i, 1.0, 0.0).astype(BF16) for i in range(LANES // head)]

    def project(a, rows, layer):
        qkv_s[pl.ds(0, rows), pl.ds(0, width)] = (dot(a, wqkv[layer, :, pl.ds(0, width)]) * scale).astype(BF16)
        qkv_s[pl.ds(0, rows), pl.ds(width, 2 * width)] = dot(a, wqkv[layer, :, pl.ds(width, 2 * width)]).astype(BF16)

    def attend(rows, masked, put):
        for j in range(pair_heads):
            q = qkv_s[pl.ds(0, rows), pl.ds(j * LANES, LANES)]
            k = qkv_s[pl.ds(0, rows), pl.ds(width + j * LANES, LANES)]
            v = qkv_s[pl.ds(0, rows), pl.ds(2 * width + j * LANES, LANES)]
            out = None
            for i in range(LANES // head):
                s = dot_nt(q, k * keep[i])
                if masked:
                    s = jnp.where(mask_s[...] > 0.5, s, MASKED)
                e = jnp.exp(s - jnp.max(s, axis=-1, keepdims=True))
                p = (e * (1.0 / jnp.sum(e, axis=-1, keepdims=True))).astype(BF16)
                part = dot(p, v * keep[i])
                out = part if out is None else out + part
            put(j, out)

    def finish(u, o, layer, rows):
        h = (u.astype(F32) + dot(o, wout[layer])).astype(BF16)
        hf = h.astype(F32)
        a2 = layer_norm(hf, norms[layer, pl.ds(2, 1), :], norms[layer, pl.ds(3, 1), :]).astype(BF16)
        chunk = 512
        for c in range(hid_s.shape[1] // chunk):
            up = dot(a2, wup[layer, :, pl.ds(c * chunk, chunk)])
            hid_s[pl.ds(0, rows), pl.ds(c * chunk, chunk)] = jax.nn.gelu(up, approximate=True).astype(BF16)
        return (hf + dot(hid_s[pl.ds(0, rows), :], wdown[layer])).astype(BF16)

    def spatial_frame(pair, v, f):
        layer = 2 * pair
        u = s_in[pair, v, f]
        a = layer_norm(u.astype(F32), norms[layer, pl.ds(0, 1), :], norms[layer, pl.ds(1, 1), :]).astype(BF16)
        project(a, patches, layer)

        def put(j, out):
            attn_s[pl.ds(0, patches), pl.ds(j * LANES, LANES)] = out.astype(BF16)

        attend(patches, False, put)
        s_out[pair, v, f] = finish(s_in[pair, v, f], attn_s[...], layer, patches)

    def send_frame(pair, v, f):
        local = pltpu.make_async_copy(s_out.at[pair, v, f, pl.ds(pl.multiple_of(me * p_loc, p_loc), p_loc), :], t_in.at[pair, v, me * f_loc + f], ac_recv.at[pair, v])
        local.start()

        def one(step, c):
            to = lax.rem(me + (n // 2) + step, n)

            pltpu.make_async_remote_copy(
                src_ref=s_out.at[pair, v, f, pl.ds(pl.multiple_of(to * p_loc, p_loc), p_loc), :],
                dst_ref=t_in.at[pair, v, me * f_loc + f],
                send_sem=ac_send.at[pair, v], recv_sem=ac_recv.at[pair, v],
                device_id={"sp": to}).start()
            return c

        def both(i, c):
            one(i, c)

            @pl.when(i > 0)
            def _():
                one(n - i, c)
            return c

        lax.fori_loop(0, n // 2, both, 0)

    def send_chunk(pair, v, to):
        src = t_out.at[pair, v, pl.ds(to * f_loc, f_loc)]
        dst = s_in.at[pair + 1, v, :, pl.ds(pl.multiple_of(me * p_loc, p_loc), p_loc), :]

        @pl.when(to == me)
        def _():
            pltpu.make_async_copy(src, dst, b_recv.at[v]).start()

        @pl.when(to != me)
        def _():
            pltpu.make_async_remote_copy(src_ref=src, dst_ref=dst, send_sem=b_send.at[v], recv_sem=b_recv.at[v], device_id={"sp": to}).start()

    def temporal(pair, v):
        layer = 2 * pair + 1
        f_chunk = frames // 4
        rows_c = f_chunk * p_loc
        to_chunk = f_chunk // f_loc

        def phase1(c, carry):
            u = t_in[pair, v, pl.ds(c * f_chunk, f_chunk)].reshape(rows_c, width).astype(F32)
            a = layer_norm(u, norms[layer, pl.ds(0, 1), :], norms[layer, pl.ds(1, 1), :])
            for j in range(pair_heads):
                a_f32[j, pl.ds(pl.multiple_of(c * rows_c, rows_c), rows_c), :] = a[:, j * LANES:(j + 1) * LANES]
            return carry

        lax.fori_loop(0, 4, phase1, 0)

        def phase2(g, carry):
            for i in range(group):
                for j in range(pair_heads):
                    attn_s[pl.ds(i * frames, frames), pl.ds(j * LANES, LANES)] = a_f32[j, pl.ds(g * group + i, frames, stride=p_loc), :].astype(BF16)
            project(attn_s[pl.ds(0, rows_g), :], rows_g, layer)

            def put(j, out):
                for i in range(group):
                    o_f32[j, pl.ds(g * group + i, frames, stride=p_loc), :] = out[i * frames:(i + 1) * frames]

            attend(rows_g, True, put)
            return carry

        lax.fori_loop(0, p_loc // group, phase2, 0)

        def phase3(i, carry):
            c = lax.rem(me // to_chunk + 2 + 3 * i + 3 * ((i * (i - 1)) // 2), 4)
            rows = pl.ds(pl.multiple_of(c * rows_c, rows_c), rows_c)
            for j in range(pair_heads):
                attn_s[pl.ds(0, rows_c), pl.ds(j * LANES, LANES)] = o_f32[j, rows, :].astype(BF16)
            u = t_in[pair, v, pl.ds(c * f_chunk, f_chunk)].reshape(rows_c, width)
            z = finish(u, attn_s[pl.ds(0, rows_c), :], layer, rows_c)
            t_out[pair, v, pl.ds(c * f_chunk, f_chunk)] = z.reshape(f_chunk, p_loc, width)

            @pl.when(pair < pairs - 1)
            def _():
                lax.fori_loop(0, to_chunk, lambda k, q: (send_chunk(pair, v, c * to_chunk + k), q)[1], 0)

            @pl.when(pair == pairs - 1)
            def _():
                pltpu.make_async_copy(t_out.at[pair, v, pl.ds(c * f_chunk, f_chunk)], y_ref.at[v, pl.ds(c * f_chunk, f_chunk)], y_sem.at[v]).start()
            return carry

        lax.fori_loop(0, 4, phase3, 0)

    def run_pair(pair, carry):
        layer = 2 * pair
        for c in weight_copies(layer):
            c.wait()
        start_weights(layer + 1)
        for v in range(videos):
            @pl.when(pair == 0)
            def _():
                pltpu.make_async_copy(x_ref.at[v], s_in.at[0, v], x_sem.at[v]).wait()

            @pl.when(pair > 0)
            def _():
                pltpu.make_async_copy(x_ref.at[v], s_in.at[1, v], b_recv.at[v]).wait()

            def frame(f, q):
                spatial_frame(pair, v, f)
                if v == 0:
                    @pl.when((f == 0) & (pair == 0))
                    def _():
                        pl.semaphore_wait(barrier, n - 1)
                send_frame(pair, v, f)
                return q

            lax.fori_loop(0, f_loc, frame, 0)
        for c in weight_copies(layer + 1):
            c.wait()

        @pl.when(pair < pairs - 1)
        def _():
            start_weights(layer + 2)

        for v in range(videos):
            pltpu.make_async_copy(t_in.at[pair, v], t_in.at[pair, v], ac_recv.at[pair, v]).wait()
            temporal(pair, v)
        return carry

    lax.fori_loop(0, pairs, run_pair, 0)

    for v in range(videos):
        pltpu.make_async_copy(y_ref.at[v], y_ref.at[v], y_sem.at[v]).wait()
        part = t_in.at[0, v, pl.ds(0, frames - f_loc)]
        for pair in range(pairs):
            pltpu.make_async_copy(part, part, ac_send.at[pair, v]).wait()
        for pair in range(pairs - 1):
            pltpu.make_async_copy(part, part, b_send.at[v]).wait()


def solution(mesh):
    n = mesh.shape["sp"]

    def local_stack(x, norms, w_qkv, w_out, w_up, w_down):
        videos, f_loc, patches, width = x.shape
        layers = w_qkv.shape[0]
        pairs = layers // 2
        head = w_qkv.shape[-1]
        hidden = w_up.shape[-1]
        frames, p_loc = f_loc * n, patches // n
        w_qkv = w_qkv.reshape(layers, width, 3 * width)
        w_out = w_out.reshape(layers, width, width)
        any_space = pl.BlockSpec(memory_space=pl.ANY)
        return pl.pallas_call(
            functools.partial(kernel, n, head),
            out_shape=jax.ShapeDtypeStruct((videos, frames, p_loc, width), BF16),
            in_specs=[any_space, pl.BlockSpec(memory_space=pltpu.VMEM)] + [any_space] * 4,
            out_specs=any_space,
            scratch_shapes=[
                pltpu.VMEM((layers, width, 3 * width), BF16),
                pltpu.VMEM((layers, width, width), BF16),
                pltpu.VMEM((layers, width, hidden), BF16),
                pltpu.VMEM((layers, hidden, width), BF16),
                pltpu.VMEM((pairs, videos, f_loc, patches, width), BF16),
                pltpu.VMEM((pairs, videos, f_loc, patches, width), BF16),
                pltpu.VMEM((pairs, videos, frames, p_loc, width), BF16),
                pltpu.VMEM((pairs, videos, frames, p_loc, width), BF16),
                pltpu.VMEM((patches, 3 * width), BF16),
                pltpu.VMEM((patches, width), BF16),
                pltpu.VMEM((patches, hidden), BF16),
                pltpu.VMEM((width // LANES, frames * p_loc, LANES), F32),
                pltpu.VMEM((width // LANES, frames * p_loc, LANES), F32),
                pltpu.VMEM((4 * frames, 4 * frames), F32),
                pltpu.SemaphoreType.DMA((layers, 4)),
                pltpu.SemaphoreType.DMA((videos,)),
                pltpu.SemaphoreType.DMA((videos,)),
                pltpu.SemaphoreType.DMA((pairs, videos)),
                pltpu.SemaphoreType.DMA((videos,)),
                pltpu.SemaphoreType.DMA((pairs, videos)),
                pltpu.SemaphoreType.DMA((videos,)),
            ],
            compiler_params=pltpu.CompilerParams(collective_id=0, has_side_effects=True, vmem_limit_bytes=60 * 1024 * 1024),
            name="stack",
        )(x, norms, w_qkv, w_out, w_up, w_down)

    replicated = P()
    return jax.shard_map(local_stack, mesh=mesh, in_specs=(P('data', 'sp', None, None), replicated, replicated, replicated, replicated, replicated), out_specs=P('data', None, 'sp', None), check_vma=False)
```

profile of v0, /device:TPU:21, one launch (start us, length us, event | category | flops | bytes accessed | tf_op | source)
XLA Modules:
  0.0 116.0 jit_solution(12822652885818810558)
XLA Ops:
  0.0 5.8 %copy.8.wqkv_hbm = bf16[4,384,1152]{2,1,0:T(8,128)(2,1)} copy(bf16[4,384,1152]{1,2,0:T(8,128)(2,1)} %bitcast.2) | data formatting | bytes 7077888 | tf_op jit(solution)/shard_map/reshape | solution.py:259
  5.8 107.9 %stack.1 = bf16[2,48,16,384]{3,2,1,0:T(8,128)(2,1)} custom-call(bf16[2,3,256,384]{3,2,1,0:T(8,128)(2,1)} %x_ref.1, f32[4,4,384]{2,1,0:T(4,128)} %norms.1, bf16[4,384,1152]{2,1,0:T(8,128)(2,1)} %copy.8.wqkv_hbm, bf16[4,384,384]{2,1,0:T(8,128)(2,1)} %bitcast.3, bf16[4,384,1536]{2,1,0:T(8,128)(2,1)} %wup_hbm.1, bf16[4,1536,384]{2,1,0:T(8,128)(2,1)} %wdown_hbm.1), custom_call_target="tpu_custom_call" | custom-call | tf_op jit(solution)/shard_map/stack/pallas_call | solution.py:262
  113.6 2.4 %copy.10 = bf16[2,48,16,384]{3,2,1,0:T(8,128)(2,1)} copy(bf16[2,48,16,384]{3,2,1,0:T(8,128)(2,1)} %stack.1) | data formatting | bytes 2359296
where the time goes:
time: 116 us
  Pallas kernels  108 us (93%)
  local copies, waits for them, and re-layouts  8.17 us (7%)
    pallas_call x1, Pallas kernels, local_stack(): pl.pallas_call(functools.partial(kernel, n, head), out_shape=jax.ShapeDty...  108 us
    reshape x1, local copies, waits for them, and re-layouts, local_stack(): w_qkv = w_qkv.reshape(layers, width, 3 * width)  5.77 us
    unnamed x1, local copies, waits for them, and re-layouts  2.4 us

commit v1 on v0

--- a/solution.py
+++ b/solution.py
@@ -10,6 +10,7 @@
 EPS = 1e-6
 LANES = 128
 MASKED = -1e38
+GELU_A, GELU_B = math.sqrt(2 / math.pi), 0.044715
 F32, BF16 = jnp.float32, jnp.bfloat16
 
 
@@ -19,6 +20,10 @@
 
 def dot_nt(a, b):
     return lax.dot_general(a, b, (((1,), (1,)), ((), ())), preferred_element_type=F32)
+
+
+def dot_tn(a, b):
+    return lax.dot_general(a, b, (((0,), (0,)), ((), ())), preferred_element_type=F32)
 
 
 def layer_norm(x, gain, shift):
@@ -28,7 +33,7 @@
 
 
 def kernel(n, head, x_ref, norms, wqkv_hbm, wout_hbm, wup_hbm, wdown_hbm, y_ref,
-           wqkv, wout, wup, wdown, s_in, s_out, t_in, t_out, qkv_s, attn_s, hid_s, a_f32, o_f32, mask_s,
+           wqkv, wout, wup, wdown, s_in, s_out, t_in, t_out, q_s, k_s, v_s, attn_s, ot_s, s_s, hid_s, a_f32, o_f32, mask_s,
            w_sem, x_sem, b_recv, ac_recv, b_send, ac_send, y_sem):
     pairs, videos, f_loc, patches, width = s_in.shape
     frames, p_loc = t_in.shape[2], t_in.shape[3]
@@ -68,37 +73,53 @@
         same = jnp.where(inside, 1.0, same)
     mask_s[...] = same
 
-    lane = lax.broadcasted_iota(jnp.int32, (1, LANES), 1)
-    keep = [jnp.where(lane // head == i, 1.0, 0.0).astype(BF16) for i in range(LANES // head)]
+    q_s[...] = jnp.zeros_like(q_s)
 
     def project(a, rows, layer):
-        qkv_s[pl.ds(0, rows), pl.ds(0, width)] = (dot(a, wqkv[layer, :, pl.ds(0, width)]) * scale).astype(BF16)
-        qkv_s[pl.ds(0, rows), pl.ds(width, 2 * width)] = dot(a, wqkv[layer, :, pl.ds(width, 2 * width)]).astype(BF16)
-
-    def attend(rows, masked, put):
-        for j in range(pair_heads):
-            q = qkv_s[pl.ds(0, rows), pl.ds(j * LANES, LANES)]
-            k = qkv_s[pl.ds(0, rows), pl.ds(width + j * LANES, LANES)]
-            v = qkv_s[pl.ds(0, rows), pl.ds(2 * width + j * LANES, LANES)]
-            out = None
-            for i in range(LANES // head):
-                s = dot_nt(q, k * keep[i])
-                if masked:
-                    s = jnp.where(mask_s[...] > 0.5, s, MASKED)
-                e = jnp.exp(s - jnp.max(s, axis=-1, keepdims=True))
-                p = (e * (1.0 / jnp.sum(e, axis=-1, keepdims=True))).astype(BF16)
-                part = dot(p, v * keep[i])
-                out = part if out is None else out + part
-            put(j, out)
+        q = (dot_nt(wqkv[layer, pl.ds(0, width), :], a) * scale).astype(BF16)
+        for h in range(width // head):
+            q_s[h, pl.ds(h * head % LANES, head), pl.ds(0, rows)] = q[h * head:(h + 1) * head]
+        k_s[pl.ds(0, rows), :] = dot_nt(a, wqkv[layer, pl.ds(width, width), :]).astype(BF16)
+        v_s[:, pl.ds(0, rows)] = dot_nt(wqkv[layer, pl.ds(2 * width, width), :], a).astype(BF16)
+
+    def attend(rows, masked):
+        heads = width // head
+        spread = math.log(rows)
+
+        def scores(h):
+            s = dot(k_s[pl.ds(0, rows), pl.ds(h * head // LANES * LANES, LANES)], q_s[h, :, pl.ds(0, rows)])
+            if masked:
+                s = jnp.where(mask_s[...] > 0.5, s, MASKED)
+            s_s[h % 2, pl.ds(0, rows), pl.ds(0, rows)] = s
+            return jnp.max(s, axis=0, keepdims=True) + spread
+
+        def mix(h, top):
+            e = jnp.exp(s_s[h % 2, pl.ds(0, rows), pl.ds(0, rows)] - top)
+            o = dot(v_s[pl.ds(h * head, head), pl.ds(0, rows)], e.astype(BF16))
+            ot_s[pl.ds(h * head, head), pl.ds(0, rows)] = (o * (1.0 / jnp.sum(e, axis=0, keepdims=True))).astype(BF16)
+
+        top = scores(0)
+        for h in range(heads):
+            later = scores(h + 1) if h + 1 < heads else None
+            mix(h, top)
+            top = later
+
+    def out_project(rows, layer):
+        return dot_tn(ot_s[:, pl.ds(0, rows)], wout[layer])
+
+    def gelu(x):
+        t = jnp.tanh(x * (GELU_A + (GELU_A * GELU_B) * (x * x)))
+        half = 0.5 * x
+        return half + half * t
 
     def finish(u, o, layer, rows):
-        h = (u.astype(F32) + dot(o, wout[layer])).astype(BF16)
+        h = (u.astype(F32) + o).astype(BF16)
         hf = h.astype(F32)
         a2 = layer_norm(hf, norms[layer, pl.ds(2, 1), :], norms[layer, pl.ds(3, 1), :]).astype(BF16)
         chunk = 512
         for c in range(hid_s.shape[1] // chunk):
             up = dot(a2, wup[layer, :, pl.ds(c * chunk, chunk)])
-            hid_s[pl.ds(0, rows), pl.ds(c * chunk, chunk)] = jax.nn.gelu(up, approximate=True).astype(BF16)
+            hid_s[pl.ds(0, rows), pl.ds(c * chunk, chunk)] = gelu(up).astype(BF16)
         return (hf + dot(hid_s[pl.ds(0, rows), :], wdown[layer])).astype(BF16)
 
     def spatial_frame(pair, v, f):
@@ -107,11 +128,8 @@
         a = layer_norm(u.astype(F32), norms[layer, pl.ds(0, 1), :], norms[layer, pl.ds(1, 1), :]).astype(BF16)
         project(a, patches, layer)
 
-        def put(j, out):
-            attn_s[pl.ds(0, patches), pl.ds(j * LANES, LANES)] = out.astype(BF16)
-
-        attend(patches, False, put)
-        s_out[pair, v, f] = finish(s_in[pair, v, f], attn_s[...], layer, patches)
+        attend(patches, False)
+        s_out[pair, v, f] = finish(s_in[pair, v, f], out_project(patches, layer), layer, patches)
 
     def send_frame(pair, v, f):
         local = pltpu.make_async_copy(s_out.at[pair, v, f, pl.ds(pl.multiple_of(me * p_loc, p_loc), p_loc), :], t_in.at[pair, v, me * f_loc + f], ac_recv.at[pair, v])
@@ -170,11 +188,11 @@
                     attn_s[pl.ds(i * frames, frames), pl.ds(j * LANES, LANES)] = a_f32[j, pl.ds(g * group + i, frames, stride=p_loc), :].astype(BF16)
             project(attn_s[pl.ds(0, rows_g), :], rows_g, layer)
 
-            def put(j, out):
-                for i in range(group):
-                    o_f32[j, pl.ds(g * group + i, frames, stride=p_loc), :] = out[i * frames:(i + 1) * frames]
-
-            attend(rows_g, True, put)
+            attend(rows_g, True)
+            o = out_project(rows_g, layer)
+            for i in range(group):
+                for j in range(pair_heads):
+                    o_f32[j, pl.ds(g * group + i, frames, stride=p_loc), :] = o[i * frames:(i + 1) * frames, j * LANES:(j + 1) * LANES]
             return carry
 
         lax.fori_loop(0, p_loc // group, phase2, 0)
@@ -182,10 +200,9 @@
         def phase3(i, carry):
             c = lax.rem(me // to_chunk + 2 + 3 * i + 3 * ((i * (i - 1)) // 2), 4)
             rows = pl.ds(pl.multiple_of(c * rows_c, rows_c), rows_c)
-            for j in range(pair_heads):
-                attn_s[pl.ds(0, rows_c), pl.ds(j * LANES, LANES)] = o_f32[j, rows, :].astype(BF16)
+            o = jnp.concatenate([o_f32[j, rows, :] for j in range(pair_heads)], axis=1)
             u = t_in[pair, v, pl.ds(c * f_chunk, f_chunk)].reshape(rows_c, width)
-            z = finish(u, attn_s[pl.ds(0, rows_c), :], layer, rows_c)
+            z = finish(u, o, layer, rows_c)
             t_out[pair, v, pl.ds(c * f_chunk, f_chunk)] = z.reshape(f_chunk, p_loc, width)
 
             @pl.when(pair < pairs - 1)
@@ -256,7 +273,7 @@
         head = w_qkv.shape[-1]
         hidden = w_up.shape[-1]
         frames, p_loc = f_loc * n, patches // n
-        w_qkv = w_qkv.reshape(layers, width, 3 * width)
+        w_qkv = w_qkv.transpose(0, 2, 3, 4, 1).reshape(layers, 3 * width, width)
         w_out = w_out.reshape(layers, width, width)
         any_space = pl.BlockSpec(memory_space=pl.ANY)
         return pl.pallas_call(
@@ -265,7 +282,7 @@
             in_specs=[any_space, pl.BlockSpec(memory_space=pltpu.VMEM)] + [any_space] * 4,
             out_specs=any_space,
             scratch_shapes=[
-                pltpu.VMEM((layers, width, 3 * width), BF16),
+                pltpu.VMEM((layers, 3 * width, width), BF16),
                 pltpu.VMEM((layers, width, width), BF16),
                 pltpu.VMEM((layers, width, hidden), BF16),
                 pltpu.VMEM((layers, hidden, width), BF16),
@@ -273,8 +290,12 @@
                 pltpu.VMEM((pairs, videos, f_loc, patches, width), BF16),
                 pltpu.VMEM((pairs, videos, frames, p_loc, width), BF16),
                 pltpu.VMEM((pairs, videos, frames, p_loc, width), BF16),
-                pltpu.VMEM((patches, 3 * width), BF16),
+                pltpu.VMEM((width // head, LANES, patches), BF16),
                 pltpu.VMEM((patches, width), BF16),
+                pltpu.VMEM((width, patches), BF16),
+                pltpu.VMEM((patches, width), BF16),
+                pltpu.VMEM((width, patches), BF16),
+                pltpu.VMEM((2, patches, patches), F32),
                 pltpu.VMEM((patches, hidden), BF16),
                 pltpu.VMEM((width // LANES, frames * p_loc, LANES), F32),
                 pltpu.VMEM((width // LANES, frames * p_loc, LANES), F32),

time: 116 us -> 110 us (0.948)
  the two profiles are of different devices: /device:TPU:21 before, /device:TPU:28 now
where the time goes in v1:
time: 110 us; the launch traced here: 109 us
  Pallas kernels  107 us (97%)
  local copies, waits for them, and re-layouts  2.4 us (2%)
    pallas_call x1, Pallas kernels, local_stack(): pl.pallas_call(functools.partial(kernel, n, head), out_shape=jax.ShapeDty...  107 us
    unnamed x1, local copies, waits for them, and re-layouts  2.4 us

profile of v1, /device:TPU:28, one launch (start us, length us, event | category | flops | bytes accessed | tf_op | source)
XLA Modules:
  0.0 109.4 jit_solution(9459647695925679609)
XLA Ops:
  0.0 106.9 %stack.1 = bf16[2,48,16,384]{3,2,1,0:T(8,128)(2,1)} custom-call(bf16[2,3,256,384]{3,2,1,0:T(8,128)(2,1)} %x_ref.1, f32[4,4,384]{2,1,0:T(4,128)} %norms.1, bf16[4,1152,384]{2,1,0:T(8,128)(2,1)} %bitcast.4, bf16[4,384,384]{2,1,0:T(8,128)(2,1)} %bitcast.5, bf16[4,384,1536]{2,1,0:T(8,128)(2,1)} %wup_hbm.1, bf16[4,1536,384]{2,1,0:T(8,128)(2,1)} %wdown_hbm.1), custom_call_target="tpu_custom_call" | custom-call | tf_op jit(solution)/shard_map/stack/pallas_call | solution.py:279
  107.0 2.4 %copy.8 = bf16[2,48,16,384]{3,2,1,0:T(8,128)(2,1)} copy(bf16[2,48,16,384]{3,2,1,0:T(8,128)(2,1)} %stack.1) | data formatting | bytes 2359296

commit v2 on v1

v2 whole, which is shorter than its diff:
```python
import functools
import math
import jax
import jax.numpy as jnp
from jax import lax
from jax.experimental import pallas as pl
from jax.experimental.pallas import tpu as pltpu
from jax.sharding import PartitionSpec as P

EPS = 1e-6
LANES = 128
SUB = 8
MASKED = -1e38
GELU_A, GELU_B = math.sqrt(2 / math.pi), 0.044715
F32, BF16 = jnp.float32, jnp.bfloat16


def dot(a, b):
    return jnp.dot(a, b, preferred_element_type=F32)


def dot_nt(a, b):
    return lax.dot_general(a, b, (((1,), (1,)), ((), ())), preferred_element_type=F32)


def dot_tn(a, b):
    return lax.dot_general(a, b, (((0,), (0,)), ((), ())), preferred_element_type=F32)


def layer_norm(x, gain, shift):
    centered = x - jnp.mean(x, axis=-1, keepdims=True)
    variance = jnp.mean(centered * centered, axis=-1, keepdims=True)
    return centered * lax.rsqrt(variance + EPS) * gain + shift


def kernel(n, head, x_ref, norms, wqkv_hbm, wout_hbm, wup_hbm, wdown_hbm, y_ref,
           wqkv, wout, wup, wdown, s_in, s_out, t_in, t_out, q_s, k_s, v_s, attn_s, ot_s, s_s, hid_s, a_f32, o_f32, mask_s,
           w_sem, x_sem, b_recv, ac_recv, b_send, ac_send, y_sem):
    pairs, videos, f_loc, tiles, sub, width = s_in.shape
    halves, frames = t_in.shape[2], t_in.shape[3]
    patches = tiles * sub
    me = lax.axis_index("sp")
    pair_heads = width // LANES
    group = 4
    rows_g = group * frames
    scale = head ** -0.5

    barrier = pltpu.get_barrier_semaphore()

    def tell(step, c):
        pl.semaphore_signal(barrier, inc=1, device_id={"sp": lax.rem(me + step, n)})
        return c

    lax.fori_loop(1, n, tell, 0)

    def weight_copies(layer):
        return [pltpu.make_async_copy(src.at[layer], dst.at[layer], w_sem.at[layer, i])
                for i, (src, dst) in enumerate(((wqkv_hbm, wqkv), (wout_hbm, wout), (wup_hbm, wup), (wdown_hbm, wdown)))]

    def start_weights(layer):
        for c in weight_copies(layer):
            c.start()

    for v in range(videos):
        pltpu.make_async_copy(x_ref.at[v], s_in.at[0, v], x_sem.at[v]).start()
    start_weights(0)

    row_p = lax.broadcasted_iota(jnp.int32, (rows_g, rows_g), 0)
    col_p = lax.broadcasted_iota(jnp.int32, (rows_g, rows_g), 1)
    same = jnp.zeros((rows_g, rows_g), F32)
    for i in range(group):
        lo, hi = i * frames, (i + 1) * frames
        inside = (row_p >= lo) & (row_p < hi) & (col_p >= lo) & (col_p < hi)
        same = jnp.where(inside, 1.0, same)
    mask_s[...] = same

    q_s[...] = jnp.zeros_like(q_s)

    def project(a, rows, layer):
        q = (dot_nt(wqkv[layer, pl.ds(0, width), :], a) * scale).astype(BF16)
        for h in range(width // head):
            q_s[h, pl.ds(h * head % LANES, head), pl.ds(0, rows)] = q[h * head:(h + 1) * head]
        k_s[pl.ds(0, rows), :] = dot_nt(a, wqkv[layer, pl.ds(width, width), :]).astype(BF16)
        v_s[:, pl.ds(0, rows)] = dot_nt(wqkv[layer, pl.ds(2 * width, width), :], a).astype(BF16)

    def attend(rows, masked):
        heads = width // head
        shift = math.log(rows)

        def scores(h):
            s = dot(k_s[pl.ds(0, rows), pl.ds(h * head // LANES * LANES, LANES)], q_s[h, :, pl.ds(0, rows)])
            if masked:
                s = jnp.where(mask_s[...] > 0.5, s, MASKED)
            s_s[h % 2, pl.ds(0, rows), pl.ds(0, rows)] = s
            return jnp.max(s, axis=0, keepdims=True) + shift

        def mix(h, top):
            e = jnp.exp(s_s[h % 2, pl.ds(0, rows), pl.ds(0, rows)] - top)
            o = dot(v_s[pl.ds(h * head, head), pl.ds(0, rows)], e.astype(BF16))
            ot_s[pl.ds(h * head, head), pl.ds(0, rows)] = (o * (1.0 / jnp.sum(e, axis=0, keepdims=True))).astype(BF16)

        top = scores(0)
        for h in range(heads):
            later = scores(h + 1) if h + 1 < heads else None
            mix(h, top)
            top = later

    def out_project(rows, layer):
        return dot_tn(ot_s[:, pl.ds(0, rows)], wout[layer])

    def gelu(x):
        t = jnp.tanh(x * (GELU_A + (GELU_A * GELU_B) * (x * x)))
        half = 0.5 * x
        return half + half * t

    def finish(u, o, layer, rows):
        h = (u + o).astype(BF16)
        hf = h.astype(F32)
        a2 = layer_norm(hf, norms[layer, pl.ds(2, 1), :], norms[layer, pl.ds(3, 1), :]).astype(BF16)
        chunk = 512
        for c in range(hid_s.shape[1] // chunk):
            up = dot(a2, wup[layer, :, pl.ds(c * chunk, chunk)])
            hid_s[pl.ds(0, rows), pl.ds(c * chunk, chunk)] = gelu(up).astype(BF16)
        return hf + dot(hid_s[pl.ds(0, rows), :], wdown[layer])

    def spatial_frame(pair, v, f):
        layer = 2 * pair
        u = s_in[pair, v, f].astype(F32).reshape(patches, width)
        a = layer_norm(u, norms[layer, pl.ds(0, 1), :], norms[layer, pl.ds(1, 1), :]).astype(BF16)
        project(a, patches, layer)

        attend(patches, False)
        u = s_in[pair, v, f].astype(F32).reshape(patches, width)
        s_out[pair, v, f] = finish(u, out_project(patches, layer), layer, patches).reshape(tiles, sub, width).astype(BF16)

    def spread(send):
        def both(i, c):
            send(lax.rem(me + n // 2 + i, n))

            @pl.when(i > 0)
            def _():
                send(lax.rem(me + n // 2 + n - i, n))
            return c

        lax.fori_loop(0, n // 2, both, 0)

    def send_frame(pair, v, f):
        def part(to):
            return s_out.at[pair, v, f, pl.ds(to * halves, halves)], t_in.at[pair, v, :, me * f_loc + f]

        def send(to):
            src, dst = part(to)
            pltpu.make_async_remote_copy(src_ref=src, dst_ref=dst, send_sem=ac_send.at[pair, v, 0], recv_sem=ac_recv.at[pair, v, 0], device_id={"sp": to}).start()

        src, dst = part(me)
        pltpu.make_async_copy(src, dst, ac_recv.at[pair, v, 0]).start()
        spread(send)

    def send_half(pair, v, h):
        def part(to):
            return s_out.at[pair, v, :, to * halves + h], t_in.at[pair, v, h, pl.ds(me * f_loc, f_loc)]

        def send(to):
            src, dst = part(to)
            pltpu.make_async_remote_copy(src_ref=src, dst_ref=dst, send_sem=ac_send.at[pair, v, h], recv_sem=ac_recv.at[pair, v, h], device_id={"sp": to}).start()

        src, dst = part(me)
        pltpu.make_async_copy(src, dst, ac_recv.at[pair, v, h]).start()
        spread(send)

    def send_chunk(pair, v, h, to):
        src = t_out.at[v, h, pl.ds(to * f_loc, f_loc)]
        dst = s_in.at[pair + 1, v, :, me * halves + h]

        @pl.when(to == me)
        def _():
            pltpu.make_async_copy(src, dst, b_recv.at[v]).start()

        @pl.when(to != me)
        def _():
            pltpu.make_async_remote_copy(src_ref=src, dst_ref=dst, send_sem=b_send.at[v, h], recv_sem=b_recv.at[v], device_id={"sp": to}).start()

    def temporal(pair, v, h):
        layer = 2 * pair + 1
        chunks = 2
        f_chunk = frames // chunks
        rows_c = f_chunk * sub
        to_chunk = f_chunk // f_loc

        def phase1(c, carry):
            u = t_in[pair, v, h, pl.ds(c * f_chunk, f_chunk)].astype(F32).reshape(rows_c, width)
            a = layer_norm(u, norms[layer, pl.ds(0, 1), :], norms[layer, pl.ds(1, 1), :])
            for j in range(pair_heads):
                a_f32[j, pl.ds(pl.multiple_of(c * rows_c, rows_c), rows_c), :] = a[:, j * LANES:(j + 1) * LANES]
            return carry

        lax.fori_loop(0, chunks, phase1, 0)

        def phase2(g, carry):
            for i in range(group):
                for j in range(pair_heads):
                    attn_s[pl.ds(i * frames, frames), pl.ds(j * LANES, LANES)] = a_f32[j, pl.ds(g * group + i, frames, stride=sub), :].astype(BF16)
            project(attn_s[pl.ds(0, rows_g), :], rows_g, layer)
            attend(rows_g, True)
            o = out_project(rows_g, layer)
            for i in range(group):
                for j in range(pair_heads):
                    o_f32[j, pl.ds(g * group + i, frames, stride=sub), :] = o[i * frames:(i + 1) * frames, j * LANES:(j + 1) * LANES]
            return carry

        lax.fori_loop(0, sub // group, phase2, 0)

        def phase3(i, carry):
            c = lax.rem(me // to_chunk + 1 + i, chunks)
            rows = pl.ds(pl.multiple_of(c * rows_c, rows_c), rows_c)
            o = jnp.concatenate([o_f32[j, rows, :] for j in range(pair_heads)], axis=1)
            u = t_in[pair, v, h, pl.ds(c * f_chunk, f_chunk)].astype(F32).reshape(rows_c, width)
            z = finish(u, o, layer, rows_c)
            t_out[v, h, pl.ds(c * f_chunk, f_chunk)] = z.reshape(f_chunk, sub, width).astype(BF16)

            @pl.when(pair < pairs - 1)
            def _():
                lax.fori_loop(0, to_chunk, lambda k, q: (send_chunk(pair, v, h, c * to_chunk + k), q)[1], 0)

            @pl.when(pair == pairs - 1)
            def _():
                pltpu.make_async_copy(t_out.at[v, h, pl.ds(c * f_chunk, f_chunk)], y_ref.at[v, pl.ds(c * f_chunk, f_chunk), h], y_sem.at[v, h]).start()
            return carry

        @pl.when(pair > 0)
        def _():
            part = t_out.at[v, h, pl.ds(0, frames - f_loc)]
            pltpu.make_async_copy(part, part, b_send.at[v, h]).wait()

        lax.fori_loop(0, chunks, phase3, 0)

    def run_pair(pair, carry):
        layer = 2 * pair
        for c in weight_copies(layer):
            c.wait()
        start_weights(layer + 1)
        for v in range(videos):
            @pl.when(pair == 0)
            def _():
                pltpu.make_async_copy(x_ref.at[v], s_in.at[0, v], x_sem.at[v]).wait()

            @pl.when(pair > 0)
            def _():
                pltpu.make_async_copy(x_ref.at[v], s_in.at[1, v], b_recv.at[v]).wait()

            def frame(f, q):
                spatial_frame(pair, v, f)
                if v == 0:
                    @pl.when((f == 0) & (pair == 0))
                    def _():
                        pl.semaphore_wait(barrier, n - 1)
                    send_frame(pair, v, f)
                return q

            lax.fori_loop(0, f_loc, frame, 0)
            if v > 0:
                for h in range(halves):
                    send_half(pair, v, h)
        for c in weight_copies(layer + 1):
            c.wait()

        @pl.when(pair < pairs - 1)
        def _():
            start_weights(layer + 2)

        for v in range(videos):
            if v == 0:
                pltpu.make_async_copy(t_in.at[pair, v], t_in.at[pair, v], ac_recv.at[pair, v, 0]).wait()

            def half(h, q):
                if v > 0:
                    pltpu.make_async_copy(t_in.at[pair, v, h], t_in.at[pair, v, h], ac_recv.at[pair, v, h]).wait()
                temporal(pair, v, h)
                return q

            lax.fori_loop(0, halves, half, 0)
        return carry

    lax.fori_loop(0, pairs, run_pair, 0)

    for v in range(videos):
        for h in range(halves):
            done = y_ref.at[v, :, h]
            pltpu.make_async_copy(done, done, y_sem.at[v, h]).wait()
            for pair in range(pairs):
                part = t_in.at[pair, v, h, pl.ds(0, frames - f_loc)]
                pltpu.make_async_copy(part, part, ac_send.at[pair, v, h if v else 0]).wait()


def solution(mesh):
    n = mesh.shape["sp"]

    def local_stack(x, norms, w_qkv, w_out, w_up, w_down):
        videos, f_loc, patches, width = x.shape
        layers = w_qkv.shape[0]
        pairs = layers // 2
        head = w_qkv.shape[-1]
        hidden = w_up.shape[-1]
        frames, halves = f_loc * n, patches // n // SUB
        x = x.reshape(videos, f_loc, patches // SUB, SUB, width)
        w_qkv = w_qkv.transpose(0, 2, 3, 4, 1).reshape(layers, 3 * width, width)
        w_out = w_out.reshape(layers, width, width)
        any_space = pl.BlockSpec(memory_space=pl.ANY)
        y = pl.pallas_call(
            functools.partial(kernel, n, head),
            out_shape=jax.ShapeDtypeStruct((videos, frames, halves, SUB, width), BF16),
            in_specs=[any_space, pl.BlockSpec(memory_space=pltpu.VMEM)] + [any_space] * 4,
            out_specs=any_space,
            scratch_shapes=[
                pltpu.VMEM((layers, 3 * width, width), BF16),
                pltpu.VMEM((layers, width, width), BF16),
                pltpu.VMEM((layers, width, hidden), BF16),
                pltpu.VMEM((layers, hidden, width), BF16),
                pltpu.VMEM((pairs, videos, f_loc, patches // SUB, SUB, width), BF16),
                pltpu.VMEM((pairs, videos, f_loc, patches // SUB, SUB, width), BF16),
                pltpu.VMEM((pairs, videos, halves, frames, SUB, width), BF16),
                pltpu.VMEM((videos, halves, frames, SUB, width), BF16),
                pltpu.VMEM((width // head, LANES, patches), BF16),
                pltpu.VMEM((patches, width), BF16),
                pltpu.VMEM((width, patches), BF16),
                pltpu.VMEM((patches, width), BF16),
                pltpu.VMEM((width, patches), BF16),
                pltpu.VMEM((2, patches, patches), F32),
                pltpu.VMEM((patches, hidden), BF16),
                pltpu.VMEM((width // LANES, frames * SUB, LANES), F32),
                pltpu.VMEM((width // LANES, frames * SUB, LANES), F32),
                pltpu.VMEM((4 * frames, 4 * frames), F32),
                pltpu.SemaphoreType.DMA((layers, 4)),
                pltpu.SemaphoreType.DMA((videos,)),
                pltpu.SemaphoreType.DMA((videos,)),
                pltpu.SemaphoreType.DMA((pairs, videos, halves)),
                pltpu.SemaphoreType.DMA((videos, halves)),
                pltpu.SemaphoreType.DMA((pairs, videos, halves)),
                pltpu.SemaphoreType.DMA((videos, halves)),
            ],
            compiler_params=pltpu.CompilerParams(collective_id=0, has_side_effects=True, vmem_limit_bytes=60 * 1024 * 1024),
            name="stack",
        )(x, norms, w_qkv, w_out, w_up, w_down)
        return y.reshape(videos, frames, halves * SUB, width)

    replicated = P()
    return jax.shard_map(local_stack, mesh=mesh, in_specs=(P('data', 'sp', None, None), replicated, replicated, replicated, replicated, replicated), out_specs=P('data', None, 'sp', None), check_vma=False)
```

time: 110 us -> 110 us (level)
  the two profiles are of different devices: /device:TPU:28 before, /device:TPU:21 now
where the time goes in v2:
time: 110 us; the launch traced here: 109 us
  Pallas kernels  106 us (96%)
  local copies, waits for them, and re-layouts  2.4 us (2%)
    pallas_call x1, Pallas kernels, local_stack(): pl.pallas_call(functools.partial(kernel, n, head), out_shape=jax.ShapeDty...  106 us
    unnamed x1, local copies, waits for them, and re-layouts  2.4 us

profile of v2, /device:TPU:21, one launch (start us, length us, event | category | flops | bytes accessed | tf_op | source)
XLA Modules:
  0.0 108.7 jit_solution(4437053049073257633)
XLA Ops:
  0.0 106.3 %stack.1 = bf16[2,48,2,8,384]{4,3,2,1,0:T(8,128)(2,1)} custom-call(bf16[2,3,32,8,384]{4,3,2,1,0:T(8,128)(2,1)} %bitcast.8, f32[4,4,384]{2,1,0:T(4,128)} %norms.1, bf16[4,1152,384]{2,1,0:T(8,128)(2,1)} %bitcast.7, bf16[4,384,384]{2,1,0:T(8,128)(2,1)} %bitcast.9, bf16[4,384,1536]{2,1,0:T(8,128)(2,1)} %wup_hbm.1, bf16[4,1536,384]{2,1,0:T(8,128)(2,1)} %wdown_hbm.1), custom_call_target="tpu_custom_call" | custom-call | tf_op jit(solution)/shard_map/stack/pallas_call | solution.py:309
  106.3 2.4 %copy.8 = bf16[2,48,16,384]{3,2,1,0:T(8,128)(2,1)} copy(bf16[2,48,16,384]{3,2,1,0:T(8,128)(2,1)} %bitcast.6) | data formatting | bytes 2359296

commit v3 on v2

--- a/solution.py
+++ b/solution.py
@@ -34,7 +34,7 @@
 
 
 def kernel(n, head, x_ref, norms, wqkv_hbm, wout_hbm, wup_hbm, wdown_hbm, y_ref,
-           wqkv, wout, wup, wdown, s_in, s_out, t_in, t_out, q_s, k_s, v_s, attn_s, ot_s, s_s, hid_s, a_f32, o_f32, mask_s,
+           wqkv, wout, wup, wdown, s_in, s_out, t_in, t_out, q_s, k_s, v_s, attn_s, ot_s, s_s, p_s, hid_s, a_f32, o_f32, mask_s,
            w_sem, x_sem, b_recv, ac_recv, b_send, ac_send, y_sem):
     pairs, videos, f_loc, tiles, sub, width = s_in.shape
     halves, frames = t_in.shape[2], t_in.shape[3]
@@ -91,19 +91,22 @@
             s = dot(k_s[pl.ds(0, rows), pl.ds(h * head // LANES * LANES, LANES)], q_s[h, :, pl.ds(0, rows)])
             if masked:
                 s = jnp.where(mask_s[...] > 0.5, s, MASKED)
-            s_s[h % 2, pl.ds(0, rows), pl.ds(0, rows)] = s
+            s_s[h, pl.ds(0, rows), pl.ds(0, rows)] = s
             return jnp.max(s, axis=0, keepdims=True) + shift
 
-        def mix(h, top):
-            e = jnp.exp(s_s[h % 2, pl.ds(0, rows), pl.ds(0, rows)] - top)
-            o = dot(v_s[pl.ds(h * head, head), pl.ds(0, rows)], e.astype(BF16))
-            ot_s[pl.ds(h * head, head), pl.ds(0, rows)] = (o * (1.0 / jnp.sum(e, axis=0, keepdims=True))).astype(BF16)
-
-        top = scores(0)
+        def weigh(h, top):
+            e = jnp.exp(s_s[h, pl.ds(0, rows), pl.ds(0, rows)] - top)
+            p_s[h, pl.ds(0, rows), pl.ds(0, rows)] = e.astype(BF16)
+            return 1.0 / jnp.sum(e, axis=0, keepdims=True)
+
+        def mix(h, norm):
+            o = dot(v_s[pl.ds(h * head, head), pl.ds(0, rows)], p_s[h, pl.ds(0, rows), pl.ds(0, rows)])
+            ot_s[pl.ds(h * head, head), pl.ds(0, rows)] = (o * norm).astype(BF16)
+
+        tops = [scores(h) for h in range(heads)]
+        norm = [weigh(h, tops[h]) for h in range(heads)]
         for h in range(heads):
-            later = scores(h + 1) if h + 1 < heads else None
-            mix(h, top)
-            top = later
+            mix(h, norm[h])
 
     def out_project(rows, layer):
         return dot_tn(ot_s[:, pl.ds(0, rows)], wout[layer])
@@ -325,7 +328,8 @@
                 pltpu.VMEM((width, patches), BF16),
                 pltpu.VMEM((patches, width), BF16),
                 pltpu.VMEM((width, patches), BF16),
-                pltpu.VMEM((2, patches, patches), F32),
+                pltpu.VMEM((width // head, patches, patches), F32),
+                pltpu.VMEM((width // head, patches, patches), BF16),
                 pltpu.VMEM((patches, hidden), BF16),
                 pltpu.VMEM((width // LANES, frames * SUB, LANES), F32),
                 pltpu.VMEM((width // LANES, frames * SUB, LANES), F32),

time: 110 us -> 106 us (0.964)
  Pallas kernels: 106 us -> 102 us
    pallas_call x1, Pallas kernels: 106 us -> 102 us  [local_stack(): pl.pallas_call(functools.partial(kernel, n, head), out_shape=jax.ShapeDty...]
where the time goes in v3:
time: 106 us; the launch traced here: 105 us
  Pallas kernels  102 us (96%)
  local copies, waits for them, and re-layouts  2.4 us (2%)
    pallas_call x1, Pallas kernels, local_stack(): pl.pallas_call(functools.partial(kernel, n, head), out_shape=jax.ShapeDty...  102 us
    unnamed x1, local copies, waits for them, and re-layouts  2.4 us

profile of v3, /device:TPU:21, one launch (start us, length us, event | category | flops | bytes accessed | tf_op | source)
XLA Modules:
  0.0 104.7 jit_solution(17489288120326520346)
XLA Ops:
  0.0 102.2 %stack.1 = bf16[2,48,2,8,384]{4,3,2,1,0:T(8,128)(2,1)} custom-call(bf16[2,3,32,8,384]{4,3,2,1,0:T(8,128)(2,1)} %bitcast.8, f32[4,4,384]{2,1,0:T(4,128)} %norms.1, bf16[4,1152,384]{2,1,0:T(8,128)(2,1)} %bitcast.7, bf16[4,384,384]{2,1,0:T(8,128)(2,1)} %bitcast.9, bf16[4,384,1536]{2,1,0:T(8,128)(2,1)} %wup_hbm.1, bf16[4,1536,384]{2,1,0:T(8,128)(2,1)} %wdown_hbm.1), custom_call_target="tpu_custom_call" | custom-call | tf_op jit(solution)/shard_map/stack/pallas_call | solution.py:312
  102.3 2.4 %copy.8 = bf16[2,48,16,384]{3,2,1,0:T(8,128)(2,1)} copy(bf16[2,48,16,384]{3,2,1,0:T(8,128)(2,1)} %bitcast.6) | data formatting | bytes 2359296

commit v4 on v3

v4 whole, which is shorter than its diff:
```python
import functools
import math
import jax
import jax.numpy as jnp
from jax import lax
from jax.experimental import pallas as pl
from jax.experimental.pallas import tpu as pltpu
from jax.sharding import PartitionSpec as P

EPS = 1e-6
LANES = 128
SUB = 8
MASKED = -1e38
GELU_A, GELU_B = math.sqrt(2 / math.pi), 0.044715
F32, BF16 = jnp.float32, jnp.bfloat16


def dot(a, b):
    return jnp.dot(a, b, preferred_element_type=F32)


def dot_nt(a, b):
    return lax.dot_general(a, b, (((1,), (1,)), ((), ())), preferred_element_type=F32)


def dot_tn(a, b):
    return lax.dot_general(a, b, (((0,), (0,)), ((), ())), preferred_element_type=F32)


def layer_norm(x, gain, shift):
    centered = x - jnp.mean(x, axis=-1, keepdims=True)
    variance = jnp.mean(centered * centered, axis=-1, keepdims=True)
    return centered * lax.rsqrt(variance + EPS) * gain + shift


def kernel(n, head, x_ref, norms, wqkv_hbm, wout_hbm, wup_hbm, wdown_hbm, y_ref,
           wqkv, wout, wup, wdown, s_in, s_out, t_in, t_out, q_s, k_s, v_s, ot_s, s_s, hid_s, next_h, next_a, cur_h, cur_a, u_f32, z_f32, mask_s,
           w_sem, x_sem, b_recv, ac_recv, b_send, ac_send, y_sem):
    pairs, videos, f_loc, tiles, sub, width = s_in.shape
    halves, frames = t_in.shape[2], t_in.shape[3]
    patches = tiles * sub
    me = lax.axis_index("sp")
    pair_heads = width // LANES
    group = 4
    rows_g = group * frames
    scale = head ** -0.5

    barrier = pltpu.get_barrier_semaphore()

    def tell(step, c):
        pl.semaphore_signal(barrier, inc=1, device_id={"sp": lax.rem(me + step, n)})
        return c

    lax.fori_loop(1, n, tell, 0)

    def weight_copies(layer):
        return [pltpu.make_async_copy(src.at[layer], dst.at[layer], w_sem.at[layer, i])
                for i, (src, dst) in enumerate(((wqkv_hbm, wqkv), (wout_hbm, wout), (wup_hbm, wup), (wdown_hbm, wdown)))]

    def start_weights(layer):
        for c in weight_copies(layer):
            c.start()

    for v in range(videos):
        pltpu.make_async_copy(x_ref.at[v], s_in.at[0, v], x_sem.at[v]).start()
    start_weights(0)

    row_p = lax.broadcasted_iota(jnp.int32, (rows_g, rows_g), 0)
    col_p = lax.broadcasted_iota(jnp.int32, (rows_g, rows_g), 1)
    same = jnp.zeros((rows_g, rows_g), F32)
    for i in range(group):
        lo, hi = i * frames, (i + 1) * frames
        inside = (row_p >= lo) & (row_p < hi) & (col_p >= lo) & (col_p < hi)
        same = jnp.where(inside, 1.0, same)
    mask_s[...] = same

    q_s[...] = jnp.zeros_like(q_s)

    heads = width // head

    def scores(h, rows, masked):
        s = dot(k_s[pl.ds(0, rows), pl.ds(h * head // LANES * LANES, LANES)], q_s[h, :, pl.ds(0, rows)])
        if masked:
            s = jnp.where(mask_s[...] > 0.5, s, MASKED)
        s_s[h, pl.ds(0, rows), pl.ds(0, rows)] = s
        return jnp.max(s, axis=0, keepdims=True) + math.log(rows)

    def mix(h, rows, top):
        e = jnp.exp(s_s[h, pl.ds(0, rows), pl.ds(0, rows)] - top)
        o = dot(v_s[pl.ds(h * head, head), pl.ds(0, rows)], e.astype(BF16))
        ot_s[pl.ds(h * head, head), pl.ds(0, rows)] = (o * (1.0 / jnp.sum(e, axis=0, keepdims=True))).astype(BF16)

    def gelu(x):
        t = jnp.tanh(x * (GELU_A + (GELU_A * GELU_B) * (x * x)))
        half = 0.5 * x
        return half + half * t

    def attention_steps(get, rows, layer, masked):
        a = layer_norm(get(), norms[layer, pl.ds(0, 1), :], norms[layer, pl.ds(1, 1), :]).astype(BF16)
        yield
        q = (dot_nt(wqkv[layer, pl.ds(0, width), :], a) * scale).astype(BF16)
        for h in range(heads):
            q_s[h, pl.ds(h * head % LANES, head), pl.ds(0, rows)] = q[h * head:(h + 1) * head]
        yield
        k_s[pl.ds(0, rows), :] = dot_nt(a, wqkv[layer, pl.ds(width, width), :]).astype(BF16)
        yield
        v_s[:, pl.ds(0, rows)] = dot_nt(wqkv[layer, pl.ds(2 * width, width), :], a).astype(BF16)
        yield
        ahead = 2
        tops = [scores(h, rows, masked) for h in range(ahead)]
        yield
        for h in range(heads):
            if h + ahead < heads:
                tops.append(scores(h + ahead, rows, masked))
            mix(h, rows, tops[h])
            yield
        h = (get() + dot_tn(ot_s[:, pl.ds(0, rows)], wout[layer])).astype(BF16)
        next_h[pl.ds(0, rows), :] = h
        next_a[pl.ds(0, rows), :] = layer_norm(h.astype(F32), norms[layer, pl.ds(2, 1), :], norms[layer, pl.ds(3, 1), :]).astype(BF16)
        yield

    def mlp_steps(rows, layer, put):
        cur_h[pl.ds(0, rows), :] = next_h[pl.ds(0, rows), :]
        cur_a[pl.ds(0, rows), :] = next_a[pl.ds(0, rows), :]
        chunk = 256
        for c in range(hid_s.shape[1] // chunk):
            up = dot(cur_a[pl.ds(0, rows), :], wup[layer, :, pl.ds(c * chunk, chunk)])
            hid_s[pl.ds(0, rows), pl.ds(c * chunk, chunk)] = gelu(up).astype(BF16)
            yield
        put(cur_h[pl.ds(0, rows), :].astype(F32) + dot(hid_s[pl.ds(0, rows), :], wdown[layer]))
        yield

    def emit(first, second):
        steps = "ABAABAABAABAABAABAB" if first is not None and second is not None else "A" * 12 + "B" * 7
        for step in steps:
            stage = first if step == "A" else second
            if stage is not None:
                next(stage)

    def pipeline(tiles_n, attention, mlp, before, after):
        before(0)
        emit(attention(0), None)

        def step(i, c):
            before(i)
            emit(attention(i), mlp(i - 1))
            after(i - 1)
            return c

        lax.fori_loop(1, tiles_n, step, 0)
        emit(None, mlp(tiles_n - 1))
        after(tiles_n - 1)

    def spread(send):
        def both(i, c):
            send(lax.rem(me + n // 2 + i, n))

            @pl.when(i > 0)
            def _():
                send(lax.rem(me + n // 2 + n - i, n))
            return c

        lax.fori_loop(0, n // 2, both, 0)

    def send_frame(pair, v, f):
        def part(to):
            return s_out.at[pair, v, f, pl.ds(to * halves, halves)], t_in.at[pair, v, :, me * f_loc + f]

        def send(to):
            src, dst = part(to)
            pltpu.make_async_remote_copy(src_ref=src, dst_ref=dst, send_sem=ac_send.at[pair, v, 0], recv_sem=ac_recv.at[pair, v, 0], device_id={"sp": to}).start()

        src, dst = part(me)
        pltpu.make_async_copy(src, dst, ac_recv.at[pair, v, 0]).start()
        spread(send)

    def send_half(pair, v, h):
        def part(to):
            return s_out.at[pair, v, :, to * halves + h], t_in.at[pair, v, h, pl.ds(me * f_loc, f_loc)]

        def send(to):
            src, dst = part(to)
            pltpu.make_async_remote_copy(src_ref=src, dst_ref=dst, send_sem=ac_send.at[pair, v, h], recv_sem=ac_recv.at[pair, v, h], device_id={"sp": to}).start()

        src, dst = part(me)
        pltpu.make_async_copy(src, dst, ac_recv.at[pair, v, h]).start()
        spread(send)

    def spatial(pair):
        layer = 2 * pair

        def before(i):
            @pl.when(lax.rem(i, f_loc) == 0)
            def _():
                v = i // f_loc

                @pl.when(pair == 0)
                def _():
                    pltpu.make_async_copy(x_ref.at[v], s_in.at[0, v], x_sem.at[v]).wait()

                @pl.when(pair > 0)
                def _():
                    pltpu.make_async_copy(x_ref.at[v], s_in.at[1, v], b_recv.at[v]).wait()

        def attention(i):
            return attention_steps(lambda: s_in[pair, i // f_loc, lax.rem(i, f_loc)].astype(F32).reshape(patches, width), patches, layer, False)

        def mlp(i):
            def put(z):
                s_out[pair, i // f_loc, lax.rem(i, f_loc)] = z.reshape(tiles, sub, width).astype(BF16)

            return mlp_steps(patches, layer, put)

        def after(i):
            v, f = i // f_loc, lax.rem(i, f_loc)

            @pl.when((pair == 0) & (i == 0))
            def _():
                pl.semaphore_wait(barrier, n - 1)

            @pl.when(v == 0)
            def _():
                send_frame(pair, v, f)

            @pl.when((v > 0) & (f == f_loc - 1))
            def _():
                for h in range(halves):
                    send_half(pair, v, h)

        pipeline(videos * f_loc, attention, mlp, before, after)

    def temporal(pair):
        layer = 2 * pair + 1
        groups = sub // group
        chunks = 2
        f_chunk = frames // chunks
        rows_c = f_chunk * sub

        def place(i):
            return i // (groups * halves), lax.rem(i // groups, halves), lax.rem(i, groups)

        def before(i):
            v, h, g = place(i)

            @pl.when(g == 0)
            def _():
                @pl.when((v == 0) & (h == 0))
                def _():
                    pltpu.make_async_copy(t_in.at[pair, 0], t_in.at[pair, 0], ac_recv.at[pair, 0, 0]).wait()

                @pl.when(v > 0)
                def _():
                    pltpu.make_async_copy(t_in.at[pair, v, h], t_in.at[pair, v, h], ac_recv.at[pair, v, h]).wait()

                def widen(c, q):
                    u = t_in[pair, v, h, pl.ds(c * f_chunk, f_chunk)].astype(F32).reshape(rows_c, width)
                    for j in range(pair_heads):
                        u_f32[j, pl.ds(pl.multiple_of(c * rows_c, rows_c), rows_c), :] = u[:, j * LANES:(j + 1) * LANES]
                    return q

                lax.fori_loop(0, chunks, widen, 0)

        def attention(i):
            g = place(i)[2]

            def get():
                return jnp.concatenate([jnp.concatenate([u_f32[j, pl.ds(g * group + p, frames, stride=sub), :] for p in range(group)], axis=0)
                                        for j in range(pair_heads)], axis=1)

            return attention_steps(get, rows_g, layer, True)

        def mlp(i):
            g = place(i)[2]

            def put(z):
                for p in range(group):
                    for j in range(pair_heads):
                        z_f32[j, pl.ds(g * group + p, frames, stride=sub), :] = z[p * frames:(p + 1) * frames, j * LANES:(j + 1) * LANES]

            return mlp_steps(rows_g, layer, put)

        def after(i):
            v, h, g = place(i)

            @pl.when(g == groups - 1)
            def _():
                @pl.when(pair > 0)
                def _():
                    part = t_out.at[v, h, pl.ds(0, frames - f_loc)]
                    pltpu.make_async_copy(part, part, b_send.at[v, h]).wait()

                def narrow(c, q):
                    rows = pl.ds(pl.multiple_of(c * rows_c, rows_c), rows_c)
                    z = jnp.concatenate([z_f32[j, rows, :] for j in range(pair_heads)], axis=1)
                    t_out[v, h, pl.ds(c * f_chunk, f_chunk)] = z.reshape(f_chunk, sub, width).astype(BF16)
                    return q

                lax.fori_loop(0, chunks, narrow, 0)

                @pl.when(pair < pairs - 1)
                def _():
                    def part(to):
                        return t_out.at[v, h, pl.ds(to * f_loc, f_loc)], s_in.at[pair + 1, v, :, me * halves + h]

                    def send(to):
                        src, dst = part(to)
                        pltpu.make_async_remote_copy(src_ref=src, dst_ref=dst, send_sem=b_send.at[v, h], recv_sem=b_recv.at[v], device_id={"sp": to}).start()

                    src, dst = part(me)
                    pltpu.make_async_copy(src, dst, b_recv.at[v]).start()
                    spread(send)

                @pl.when(pair == pairs - 1)
                def _():
                    pltpu.make_async_copy(t_out.at[v, h], y_ref.at[v, :, h], y_sem.at[v, h]).start()

        pipeline(videos * halves * groups, attention, mlp, before, after)

    def run_pair(pair, carry):
        layer = 2 * pair
        for c in weight_copies(layer):
            c.wait()
        start_weights(layer + 1)
        spatial(pair)
        for c in weight_copies(layer + 1):
            c.wait()

        @pl.when(pair < pairs - 1)
        def _():
            start_weights(layer + 2)

        temporal(pair)
        return carry

    lax.fori_loop(0, pairs, run_pair, 0)

    for v in range(videos):
        for h in range(halves):
            done = y_ref.at[v, :, h]
            pltpu.make_async_copy(done, done, y_sem.at[v, h]).wait()
            for pair in range(pairs):
                part = t_in.at[pair, v, h, pl.ds(0, frames - f_loc)]
                pltpu.make_async_copy(part, part, ac_send.at[pair, v, h if v else 0]).wait()


def solution(mesh):
    n = mesh.shape["sp"]

    def local_stack(x, norms, w_qkv, w_out, w_up, w_down):
        videos, f_loc, patches, width = x.shape
        layers = w_qkv.shape[0]
        pairs = layers // 2
        head = w_qkv.shape[-1]
        hidden = w_up.shape[-1]
        frames, halves = f_loc * n, patches // n // SUB
        x = x.reshape(videos, f_loc, patches // SUB, SUB, width)
        w_qkv = w_qkv.transpose(0, 2, 3, 4, 1).reshape(layers, 3 * width, width)
        w_out = w_out.reshape(layers, width, width)
        any_space = pl.BlockSpec(memory_space=pl.ANY)
        y = pl.pallas_call(
            functools.partial(kernel, n, head),
            out_shape=jax.ShapeDtypeStruct((videos, frames, halves, SUB, width), BF16),
            in_specs=[any_space, pl.BlockSpec(memory_space=pltpu.VMEM)] + [any_space] * 4,
            out_specs=any_space,
            scratch_shapes=[
                pltpu.VMEM((layers, 3 * width, width), BF16),
                pltpu.VMEM((layers, width, width), BF16),
                pltpu.VMEM((layers, width, hidden), BF16),
                pltpu.VMEM((layers, hidden, width), BF16),
                pltpu.VMEM((pairs, videos, f_loc, patches // SUB, SUB, width), BF16),
                pltpu.VMEM((pairs, videos, f_loc, patches // SUB, SUB, width), BF16),
                pltpu.VMEM((pairs, videos, halves, frames, SUB, width), BF16),
                pltpu.VMEM((videos, halves, frames, SUB, width), BF16),
                pltpu.VMEM((width // head, LANES, patches), BF16),
                pltpu.VMEM((patches, width), BF16),
                pltpu.VMEM((width, patches), BF16),
                pltpu.VMEM((width, patches), BF16),
                pltpu.VMEM((width // head, patches, patches), F32),
                pltpu.VMEM((patches, hidden), BF16),
                pltpu.VMEM((patches, width), BF16),
                pltpu.VMEM((patches, width), BF16),
                pltpu.VMEM((patches, width), BF16),
                pltpu.VMEM((patches, width), BF16),
                pltpu.VMEM((width // LANES, frames * SUB, LANES), F32),
                pltpu.VMEM((width // LANES, frames * SUB, LANES), F32),
                pltpu.VMEM((4 * frames, 4 * frames), F32),
                pltpu.SemaphoreType.DMA((layers, 4)),
                pltpu.SemaphoreType.DMA((videos,)),
                pltpu.SemaphoreType.DMA((videos,)),
                pltpu.SemaphoreType.DMA((pairs, videos, halves)),
                pltpu.SemaphoreType.DMA((videos, halves)),
                pltpu.SemaphoreType.DMA((pairs, videos, halves)),
                pltpu.SemaphoreType.DMA((videos, halves)),
            ],
            compiler_params=pltpu.CompilerParams(collective_id=0, has_side_effects=True, vmem_limit_bytes=60 * 1024 * 1024),
            name="stack",
        )(x, norms, w_qkv, w_out, w_up, w_down)
        return y.reshape(videos, frames, halves * SUB, width)

    replicated = P()
    return jax.shard_map(local_stack, mesh=mesh, in_specs=(P('data', 'sp', None, None), replicated, replicated, replicated, replicated, replicated), out_specs=P('data', None, 'sp', None), check_vma=False)
```

time: 106 us -> 109 us (1.028); the launches traced: 105 us -> 109 us
  Pallas kernels: 102 us -> 107 us
    pallas_call x1, Pallas kernels: 102 us -> 107 us  [local_stack(): pl.pallas_call(functools.partial(kernel, n, head), out_shape=jax.ShapeDty...]
where the time goes in v4:
time: 109 us
  Pallas kernels  107 us (98%)
  local copies, waits for them, and re-layouts  2.4 us (2%)
    pallas_call x1, Pallas kernels, local_stack(): pl.pallas_call(functools.partial(kernel, n, head), out_shape=jax.ShapeDty...  107 us
    unnamed x1, local copies, waits for them, and re-layouts  2.4 us

profile of v4, /device:TPU:21, one launch (start us, length us, event | category | flops | bytes accessed | tf_op | source)
XLA Modules:
  0.0 109.0 jit_solution(10981460196204433258)
XLA Ops:
  0.0 106.6 %stack.1 = bf16[2,48,2,8,384]{4,3,2,1,0:T(8,128)(2,1)} custom-call(bf16[2,3,32,8,384]{4,3,2,1,0:T(8,128)(2,1)} %bitcast.8, f32[4,4,384]{2,1,0:T(4,128)} %norms.1, bf16[4,1152,384]{2,1,0:T(8,128)(2,1)} %bitcast.7, bf16[4,384,384]{2,1,0:T(8,128)(2,1)} %bitcast.9, bf16[4,384,1536]{2,1,0:T(8,128)(2,1)} %wup_hbm.1, bf16[4,1536,384]{2,1,0:T(8,128)(2,1)} %wdown_hbm.1), custom_call_target="tpu_custom_call" | custom-call | tf_op jit(solution)/shard_map/stack/pallas_call | solution.py:360
  106.6 2.4 %copy.8 = bf16[2,48,16,384]{3,2,1,0:T(8,128)(2,1)} copy(bf16[2,48,16,384]{3,2,1,0:T(8,128)(2,1)} %bitcast.6) | data formatting | bytes 2359296

commit v5 on v4

--- a/solution.py
+++ b/solution.py
@@ -10,7 +10,7 @@
 EPS = 1e-6
 LANES = 128
 SUB = 8
-MASKED = -1e38
+VMEM_BYTES = 65_700_000
 GELU_A, GELU_B = math.sqrt(2 / math.pi), 0.044715
 F32, BF16 = jnp.float32, jnp.bfloat16
 
@@ -67,28 +67,48 @@
 
     row_p = lax.broadcasted_iota(jnp.int32, (rows_g, rows_g), 0)
     col_p = lax.broadcasted_iota(jnp.int32, (rows_g, rows_g), 1)
-    same = jnp.zeros((rows_g, rows_g), F32)
+    across = jnp.full((rows_g, rows_g), -jnp.inf, F32)
     for i in range(group):
         lo, hi = i * frames, (i + 1) * frames
         inside = (row_p >= lo) & (row_p < hi) & (col_p >= lo) & (col_p < hi)
-        same = jnp.where(inside, 1.0, same)
-    mask_s[...] = same
-
+        across = jnp.where(inside, 0.0, across)
+    mask_s[...] = across
     q_s[...] = jnp.zeros_like(q_s)
 
     heads = width // head
+
+    def strips(rows, masked):
+        out = []
+        for lo in range(0, rows, LANES):
+            hi = min(rows, lo + LANES)
+            out.append((lo, hi, lo // frames * frames, -(-hi // frames) * frames) if masked else (lo, hi, 0, rows))
+        return out if masked else [(0, rows, 0, rows)]
 
     def scores(h, rows, masked):
         s = dot(k_s[pl.ds(0, rows), pl.ds(h * head // LANES * LANES, LANES)], q_s[h, :, pl.ds(0, rows)])
-        if masked:
-            s = jnp.where(mask_s[...] > 0.5, s, MASKED)
-        s_s[h, pl.ds(0, rows), pl.ds(0, rows)] = s
-        return jnp.max(s, axis=0, keepdims=True) + math.log(rows)
-
-    def mix(h, rows, top):
-        e = jnp.exp(s_s[h, pl.ds(0, rows), pl.ds(0, rows)] - top)
-        o = dot(v_s[pl.ds(h * head, head), pl.ds(0, rows)], e.astype(BF16))
-        ot_s[pl.ds(h * head, head), pl.ds(0, rows)] = (o * (1.0 / jnp.sum(e, axis=0, keepdims=True))).astype(BF16)
+        tops = []
+        for lo, hi, k0, k1 in strips(rows, masked):
+            part = s[k0:k1, lo:hi]
+            if masked:
+                part = part + mask_s[pl.ds(k0, k1 - k0), pl.ds(lo, hi - lo)]
+            s_s[h, pl.ds(k0, k1 - k0), pl.ds(lo, hi - lo)] = part
+            tops.append(jnp.max(part, axis=0, keepdims=True) + math.log(rows))
+        return tops
+
+    def mix(h, rows, masked, tops):
+        cols, sums = [], []
+        for (lo, hi, k0, k1), top in zip(strips(rows, masked), tops):
+            e = jnp.exp(s_s[h, pl.ds(k0, k1 - k0), pl.ds(lo, hi - lo)] - top)
+            sums.append(jnp.sum(e, axis=0, keepdims=True))
+            col = [jnp.zeros((k, hi - lo), BF16) for k in (k0,)] if k0 else []
+            col.append(e.astype(BF16))
+            if k1 < rows:
+                col.append(jnp.zeros((rows - k1, hi - lo), BF16))
+            cols.append(jnp.concatenate(col, axis=0) if len(col) > 1 else col[0])
+        p = jnp.concatenate(cols, axis=1) if len(cols) > 1 else cols[0]
+        norm = jnp.concatenate(sums, axis=1) if len(sums) > 1 else sums[0]
+        o = dot(v_s[pl.ds(h * head, head), pl.ds(0, rows)], p)
+        ot_s[pl.ds(h * head, head), pl.ds(0, rows)] = (o * (1.0 / norm)).astype(BF16)
 
     def gelu(x):
         t = jnp.tanh(x * (GELU_A + (GELU_A * GELU_B) * (x * x)))
@@ -112,7 +132,7 @@
         for h in range(heads):
             if h + ahead < heads:
                 tops.append(scores(h + ahead, rows, masked))
-            mix(h, rows, tops[h])
+            mix(h, rows, masked, tops[h])
             yield
         h = (get() + dot_tn(ot_s[:, pl.ds(0, rows)], wout[layer])).astype(BF16)
         next_h[pl.ds(0, rows), :] = h
@@ -359,9 +379,9 @@
         any_space = pl.BlockSpec(memory_space=pl.ANY)
         y = pl.pallas_call(
             functools.partial(kernel, n, head),
-            out_shape=jax.ShapeDtypeStruct((videos, frames, halves, SUB, width), BF16),
+            out_shape=pltpu.VMEM((videos, frames, halves, SUB, width), BF16),
             in_specs=[any_space, pl.BlockSpec(memory_space=pltpu.VMEM)] + [any_space] * 4,
-            out_specs=any_space,
+            out_specs=pl.BlockSpec(memory_space=pltpu.VMEM),
             scratch_shapes=[
                 pltpu.VMEM((layers, 3 * width, width), BF16),
                 pltpu.VMEM((layers, width, width), BF16),
@@ -392,7 +412,7 @@
                 pltpu.SemaphoreType.DMA((pairs, videos, halves)),
                 pltpu.SemaphoreType.DMA((videos, halves)),
             ],
-            compiler_params=pltpu.CompilerParams(collective_id=0, has_side_effects=True, vmem_limit_bytes=60 * 1024 * 1024),
+            compiler_params=pltpu.CompilerParams(collective_id=0, has_side_effects=True, vmem_limit_bytes=VMEM_BYTES),
             name="stack",
         )(x, norms, w_qkv, w_out, w_up, w_down)
         return y.reshape(videos, frames, halves * SUB, width)

time: 109 us -> 102 us (0.936)
  Pallas kernels: 107 us -> 101 us
  local copies, waits for them, and re-layouts: 2.4 us -> 1.02 us
    pallas_call x1, Pallas kernels: 107 us -> 101 us  [local_stack(): pl.pallas_call(functools.partial(kernel, n, head), out_shape=pltpu.VMEM((...]
    unnamed x1, local copies, waits for them, and re-layouts: 2.4 us -> 1.02 us
where the time goes in v5:
time: 102 us
  Pallas kernels  101 us (99%)
  local copies, waits for them, and re-layouts  1.02 us (1%)
    pallas_call x1, Pallas kernels, local_stack(): pl.pallas_call(functools.partial(kernel, n, head), out_shape=pltpu.VMEM((...  101 us

profile of v5, /device:TPU:21, one launch (start us, length us, event | category | flops | bytes accessed | tf_op | source)
XLA Modules:
  0.0 101.8 jit_solution(14592680885848407281)
XLA Ops:
  0.0 100.8 %stack.1 = bf16[2,48,2,8,384]{4,3,2,1,0:T(8,128)(2,1)S(1)} custom-call(bf16[2,3,32,8,384]{4,3,2,1,0:T(8,128)(2,1)} %bitcast.8, f32[4,4,384]{2,1,0:T(4,128)} %norms.1, bf16[4,1152,384]{2,1,0:T(8,128)(2,1)} %bitcast.7, bf16[4,384,384]{2,1,0:T(8,128)(2,1)} %bitcast.9, bf16[4,384,1536]{2,1,0:T(8,128)(2,1)} %wup_hbm.1, bf16[4,1536,384]{2,1,0:T(8,128)(2,1)} %wdown_hbm.1), custom_call_target="tpu_custom_call" | custom-call | tf_op jit(solution)/shard_map/stack/pallas_call | solution.py:380
  100.8 1.0 copy.8

commit v6 on v5

--- a/solution.py
+++ b/solution.py
@@ -11,6 +11,7 @@
 LANES = 128
 SUB = 8
 VMEM_BYTES = 65_700_000
+ATTENTION_STEPS, MLP_STEPS = 12, 7
 GELU_A, GELU_B = math.sqrt(2 / math.pi), 0.044715
 F32, BF16 = jnp.float32, jnp.bfloat16
 
@@ -53,13 +54,19 @@
 
     lax.fori_loop(1, n, tell, 0)
 
-    def weight_copies(layer):
-        return [pltpu.make_async_copy(src.at[layer], dst.at[layer], w_sem.at[layer, i])
-                for i, (src, dst) in enumerate(((wqkv_hbm, wqkv), (wout_hbm, wout), (wup_hbm, wup), (wdown_hbm, wdown)))]
+    weights = ((wqkv_hbm, wqkv), (wout_hbm, wout), (wup_hbm, wup), (wdown_hbm, wdown))
+
+    def weight_copy(layer, i):
+        src, dst = weights[i]
+        return pltpu.make_async_copy(src.at[layer], dst.at[layer], w_sem.at[layer, i])
 
     def start_weights(layer):
-        for c in weight_copies(layer):
-            c.start()
+        for i in range(len(weights)):
+            weight_copy(layer, i).start()
+
+    def wait_weights(layer, which):
+        for i in which:
+            weight_copy(layer, i).wait()
 
     for v in range(videos):
         pltpu.make_async_copy(x_ref.at[v], s_in.at[0, v], x_sem.at[v]).start()
@@ -151,23 +158,35 @@
         yield
 
     def emit(first, second):
-        steps = "ABAABAABAABAABAABAB" if first is not None and second is not None else "A" * 12 + "B" * 7
+        steps = "ABAABAABAABAABAABAB" if first is not None and second is not None else "A" * ATTENTION_STEPS + "B" * MLP_STEPS
         for step in steps:
             stage = first if step == "A" else second
             if stage is not None:
                 next(stage)
 
-    def pipeline(tiles_n, attention, mlp, before, after):
-        before(0)
-        emit(attention(0), None)
+    def pipeline(tiles_n, attention, mlp, after, alone=None, late=None):
+        steps = attention(0)
+        for _ in range(ATTENTION_STEPS - 1):
+            next(steps)
+        if late is not None:
+            late()
+        next(steps)
+        start = 1
+        if alone is not None:
+            @pl.when(alone)
+            def _():
+                emit(None, mlp(0))
+                after(0)
+                emit(attention(1), None)
+
+            start = jnp.where(alone, 2, 1)
 
         def step(i, c):
-            before(i)
             emit(attention(i), mlp(i - 1))
             after(i - 1)
             return c
 
-        lax.fori_loop(1, tiles_n, step, 0)
+        lax.fori_loop(start, tiles_n, step, 0)
         emit(None, mlp(tiles_n - 1))
         after(tiles_n - 1)
 
@@ -209,45 +228,48 @@
     def spatial(pair):
         layer = 2 * pair
 
-        def before(i):
-            @pl.when(lax.rem(i, f_loc) == 0)
-            def _():
-                v = i // f_loc
-
-                @pl.when(pair == 0)
+        def video(v, c):
+            @pl.when(pair == 0)
+            def _():
+                pltpu.make_async_copy(x_ref.at[v], s_in.at[0, v], x_sem.at[v]).wait()
+
+            @pl.when(pair > 0)
+            def _():
+                pltpu.make_async_copy(x_ref.at[v], s_in.at[1, v], b_recv.at[v]).wait()
+
+            def attention(f):
+                return attention_steps(lambda: s_in[pair, v, f].astype(F32).reshape(patches, width), patches, layer, False)
+
+            def mlp(f):
+                def put(z):
+                    s_out[pair, v, f] = z.reshape(tiles, sub, width).astype(BF16)
+
+                return mlp_steps(patches, layer, put)
+
+            def after(f):
+                @pl.when((pair == 0) & (v == 0) & (f == 0))
                 def _():
-                    pltpu.make_async_copy(x_ref.at[v], s_in.at[0, v], x_sem.at[v]).wait()
-
-                @pl.when(pair > 0)
+                    pl.semaphore_wait(barrier, n - 1)
+
+                @pl.when(v == 0)
                 def _():
-                    pltpu.make_async_copy(x_ref.at[v], s_in.at[1, v], b_recv.at[v]).wait()
-
-        def attention(i):
-            return attention_steps(lambda: s_in[pair, i // f_loc, lax.rem(i, f_loc)].astype(F32).reshape(patches, width), patches, layer, False)
-
-        def mlp(i):
-            def put(z):
-                s_out[pair, i // f_loc, lax.rem(i, f_loc)] = z.reshape(tiles, sub, width).astype(BF16)
-
-            return mlp_steps(patches, layer, put)
-
-        def after(i):
-            v, f = i // f_loc, lax.rem(i, f_loc)
-
-            @pl.when((pair == 0) & (i == 0))
-            def _():
-                pl.semaphore_wait(barrier, n - 1)
-
-            @pl.when(v == 0)
-            def _():
-                send_frame(pair, v, f)
-
-            @pl.when((v > 0) & (f == f_loc - 1))
-            def _():
-                for h in range(halves):
-                    send_half(pair, v, h)
-
-        pipeline(videos * f_loc, attention, mlp, before, after)
+                    send_frame(pair, v, f)
+
+                @pl.when((v > 0) & (f == f_loc - 1))
+                def _():
+                    for h in range(halves):
+                        send_half(pair, v, h)
+
+            def late():
+                @pl.when(v == 0)
+                def _():
+                    wait_weights(layer, (1, 2, 3))
+                    start_weights(layer + 1)
+
+            pipeline(f_loc, attention, mlp, after, (pair == 0) & (v == 0), late)
+            return c
+
+        lax.fori_loop(0, videos, video, 0)
 
     def temporal(pair):
         layer = 2 * pair + 1
@@ -256,42 +278,36 @@
         f_chunk = frames // chunks
         rows_c = f_chunk * sub
 
-        def place(i):
-            return i // (groups * halves), lax.rem(i // groups, halves), lax.rem(i, groups)
-
-        def before(i):
-            v, h, g = place(i)
-
-            @pl.when(g == 0)
-            def _():
-                @pl.when((v == 0) & (h == 0))
-                def _():
-                    pltpu.make_async_copy(t_in.at[pair, 0], t_in.at[pair, 0], ac_recv.at[pair, 0, 0]).wait()
-
-                @pl.when(v > 0)
-                def _():
-                    pltpu.make_async_copy(t_in.at[pair, v, h], t_in.at[pair, v, h], ac_recv.at[pair, v, h]).wait()
-
-                def widen(c, q):
-                    u = t_in[pair, v, h, pl.ds(c * f_chunk, f_chunk)].astype(F32).reshape(rows_c, width)
-                    for j in range(pair_heads):
-                        u_f32[j, pl.ds(pl.multiple_of(c * rows_c, rows_c), rows_c), :] = u[:, j * LANES:(j + 1) * LANES]
-                    return q
-
-                lax.fori_loop(0, chunks, widen, 0)
-
-        def attention(i):
-            g = place(i)[2]
-
+        def unit(i, carry):
+            v, h = i // halves, lax.rem(i, halves)
+
+            @pl.when((v == 0) & (h == 0))
+            def _():
+                pltpu.make_async_copy(t_in.at[pair, 0], t_in.at[pair, 0], ac_recv.at[pair, 0, 0]).wait()
+
+            @pl.when(v > 0)
+            def _():
+                pltpu.make_async_copy(t_in.at[pair, v, h], t_in.at[pair, v, h], ac_recv.at[pair, v, h]).wait()
+
+            def widen(c, q):
+                u = t_in[pair, v, h, pl.ds(c * f_chunk, f_chunk)].astype(F32).reshape(rows_c, width)
+                for j in range(pair_heads):
+                    u_f32[j, pl.ds(pl.multiple_of(c * rows_c, rows_c), rows_c), :] = u[:, j * LANES:(j + 1) * LANES]
+                return q
+
+            lax.fori_loop(0, chunks, widen, 0)
+            pipeline(groups, attention, mlp, lambda g: None)
+            finish(v, h)
+            return carry
+
+        def attention(g):
             def get():
                 return jnp.concatenate([jnp.concatenate([u_f32[j, pl.ds(g * group + p, frames, stride=sub), :] for p in range(group)], axis=0)
                                         for j in range(pair_heads)], axis=1)
 
             return attention_steps(get, rows_g, layer, True)
 
-        def mlp(i):
-            g = place(i)[2]
-
+        def mlp(g):
             def put(z):
                 for p in range(group):
                     for j in range(pair_heads):
@@ -299,51 +315,44 @@
 
             return mlp_steps(rows_g, layer, put)
 
-        def after(i):
-            v, h, g = place(i)
-
-            @pl.when(g == groups - 1)
-            def _():
-                @pl.when(pair > 0)
-                def _():
-                    part = t_out.at[v, h, pl.ds(0, frames - f_loc)]
-                    pltpu.make_async_copy(part, part, b_send.at[v, h]).wait()
-
-                def narrow(c, q):
-                    rows = pl.ds(pl.multiple_of(c * rows_c, rows_c), rows_c)
-                    z = jnp.concatenate([z_f32[j, rows, :] for j in range(pair_heads)], axis=1)
-                    t_out[v, h, pl.ds(c * f_chunk, f_chunk)] = z.reshape(f_chunk, sub, width).astype(BF16)
-                    return q
-
-                lax.fori_loop(0, chunks, narrow, 0)
-
-                @pl.when(pair < pairs - 1)
-                def _():
-                    def part(to):
-                        return t_out.at[v, h, pl.ds(to * f_loc, f_loc)], s_in.at[pair + 1, v, :, me * halves + h]
-
-                    def send(to):
-                        src, dst = part(to)
-                        pltpu.make_async_remote_copy(src_ref=src, dst_ref=dst, send_sem=b_send.at[v, h], recv_sem=b_recv.at[v], device_id={"sp": to}).start()
-
-                    src, dst = part(me)
-                    pltpu.make_async_copy(src, dst, b_recv.at[v]).start()
-                    spread(send)
-
-                @pl.when(pair == pairs - 1)
-                def _():
-                    pltpu.make_async_copy(t_out.at[v, h], y_ref.at[v, :, h], y_sem.at[v, h]).start()
-
-        pipeline(videos * halves * groups, attention, mlp, before, after)
+        def finish(v, h):
+            @pl.when(pair > 0)
+            def _():
+                part = t_out.at[v, h, pl.ds(0, frames - f_loc)]
+                pltpu.make_async_copy(part, part, b_send.at[v, h]).wait()
+
+            def narrow(c, q):
+                rows = pl.ds(pl.multiple_of(c * rows_c, rows_c), rows_c)
+                z = jnp.concatenate([z_f32[j, rows, :] for j in range(pair_heads)], axis=1)
+                t_out[v, h, pl.ds(c * f_chunk, f_chunk)] = z.reshape(f_chunk, sub, width).astype(BF16)
+                return q
+
+            lax.fori_loop(0, chunks, narrow, 0)
+
+            @pl.when(pair < pairs - 1)
+            def _():
+                def part(to):
+                    return t_out.at[v, h, pl.ds(to * f_loc, f_loc)], s_in.at[pair + 1, v, :, me * halves + h]
+
+                def send(to):
+                    src, dst = part(to)
+                    pltpu.make_async_remote_copy(src_ref=src, dst_ref=dst, send_sem=b_send.at[v, h], recv_sem=b_recv.at[v], device_id={"sp": to}).start()
+
+                src, dst = part(me)
+                pltpu.make_async_copy(src, dst, b_recv.at[v]).start()
+                spread(send)
+
+            @pl.when(pair == pairs - 1)
+            def _():
+                pltpu.make_async_copy(t_out.at[v, h], y_ref.at[v, :, h], y_sem.at[v, h]).start()
+
+        lax.fori_loop(0, videos * halves, unit, 0)
 
     def run_pair(pair, carry):
         layer = 2 * pair
-        for c in weight_copies(layer):
-            c.wait()
-        start_weights(layer + 1)
+        wait_weights(layer, (0,))
         spatial(pair)
-        for c in weight_copies(layer + 1):
-            c.wait()
+        wait_weights(layer + 1, range(len(weights)))
 
         @pl.when(pair < pairs - 1)
         def _():

time: 102 us -> 101 us (level)
  the two profiles are of different devices: /device:TPU:21 before, /device:TPU:22 now
where the time goes in v6:
time: 101 us; the launch traced here: 100 us
  Pallas kernels  99.4 us (98%)
  local copies, waits for them, and re-layouts  1.02 us (1%)
    pallas_call x1, Pallas kernels, local_stack(): pl.pallas_call(functools.partial(kernel, n, head), out_shape=pltpu.VMEM((...  99.4 us

profile of v6, /device:TPU:22, one launch (start us, length us, event | category | flops | bytes accessed | tf_op | source)
XLA Modules:
  0.0 100.4 jit_solution(14984816073918629860)
XLA Ops:
  0.0 99.4 %stack.1 = bf16[2,48,2,8,384]{4,3,2,1,0:T(8,128)(2,1)S(1)} custom-call(bf16[2,3,32,8,384]{4,3,2,1,0:T(8,128)(2,1)} %bitcast.8, f32[4,4,384]{2,1,0:T(4,128)} %norms.1, bf16[4,1152,384]{2,1,0:T(8,128)(2,1)} %bitcast.7, bf16[4,384,384]{2,1,0:T(8,128)(2,1)} %bitcast.9, bf16[4,384,1536]{2,1,0:T(8,128)(2,1)} %wup_hbm.1, bf16[4,1536,384]{2,1,0:T(8,128)(2,1)} %wdown_hbm.1), custom_call_target="tpu_custom_call" | custom-call | tf_op jit(solution)/shard_map/stack/pallas_call | solution.py:389
  99.4 1.0 %copy.8 = bf16[2,48,16,384]{3,2,1,0:T(8,128)(2,1)} copy(bf16[2,48,16,384]{3,2,1,0:T(8,128)(2,1)S(1)} %bitcast.6) | data formatting | bytes 2359296

commit v7 on v6

--- a/solution.py
+++ b/solution.py
@@ -36,7 +36,7 @@
 
 def kernel(n, head, x_ref, norms, wqkv_hbm, wout_hbm, wup_hbm, wdown_hbm, y_ref,
            wqkv, wout, wup, wdown, s_in, s_out, t_in, t_out, q_s, k_s, v_s, ot_s, s_s, hid_s, next_h, next_a, cur_h, cur_a, u_f32, z_f32, mask_s,
-           w_sem, x_sem, b_recv, ac_recv, b_send, ac_send, y_sem):
+           w_sem, x_sem, b_recv, ac_recv, b_send, ac_send):
     pairs, videos, f_loc, tiles, sub, width = s_in.shape
     halves, frames = t_in.shape[2], t_in.shape[3]
     patches = tiles * sub
@@ -46,6 +46,23 @@
     rows_g = group * frames
     scale = head ** -0.5
 
+    weights = ((wqkv_hbm, wqkv), (wout_hbm, wout), (wup_hbm, wup), (wdown_hbm, wdown))
+
+    def weight_copy(layer, i):
+        src, dst = weights[i]
+        return pltpu.make_async_copy(src.at[layer], dst.at[layer], w_sem.at[layer, i])
+
+    def start_weights(layer, first=0):
+        for i in range(first, len(weights)):
+            weight_copy(layer, i).start()
+
+    def wait_weights(layer, which):
+        for i in which:
+            weight_copy(layer, i).wait()
+
+    pltpu.make_async_copy(x_ref.at[0], s_in.at[0, 0], x_sem.at[0]).start()
+    weight_copy(0, 0).start()
+
     barrier = pltpu.get_barrier_semaphore()
 
     def tell(step, c):
@@ -54,23 +71,6 @@
 
     lax.fori_loop(1, n, tell, 0)
 
-    weights = ((wqkv_hbm, wqkv), (wout_hbm, wout), (wup_hbm, wup), (wdown_hbm, wdown))
-
-    def weight_copy(layer, i):
-        src, dst = weights[i]
-        return pltpu.make_async_copy(src.at[layer], dst.at[layer], w_sem.at[layer, i])
-
-    def start_weights(layer):
-        for i in range(len(weights)):
-            weight_copy(layer, i).start()
-
-    def wait_weights(layer, which):
-        for i in which:
-            weight_copy(layer, i).wait()
-
-    for v in range(videos):
-        pltpu.make_async_copy(x_ref.at[v], s_in.at[0, v], x_sem.at[v]).start()
-    start_weights(0)
 
     row_p = lax.broadcasted_iota(jnp.int32, (rows_g, rows_g), 0)
     col_p = lax.broadcasted_iota(jnp.int32, (rows_g, rows_g), 1)
@@ -191,15 +191,10 @@
         after(tiles_n - 1)
 
     def spread(send):
-        def both(i, c):
+        for i in range(n // 2):
             send(lax.rem(me + n // 2 + i, n))
-
-            @pl.when(i > 0)
-            def _():
+            if i > 0:
                 send(lax.rem(me + n // 2 + n - i, n))
-            return c
-
-        lax.fori_loop(0, n // 2, both, 0)
 
     def send_frame(pair, v, f):
         def part(to):
@@ -235,7 +230,7 @@
 
             @pl.when(pair > 0)
             def _():
-                pltpu.make_async_copy(x_ref.at[v], s_in.at[1, v], b_recv.at[v]).wait()
+                pltpu.make_async_copy(x_ref.at[v], s_in.at[pair, v], b_recv.at[pair - 1, v]).wait()
 
             def attention(f):
                 return attention_steps(lambda: s_in[pair, v, f].astype(F32).reshape(patches, width), patches, layer, False)
@@ -316,15 +311,18 @@
             return mlp_steps(rows_g, layer, put)
 
         def finish(v, h):
-            @pl.when(pair > 0)
-            def _():
-                part = t_out.at[v, h, pl.ds(0, frames - f_loc)]
-                pltpu.make_async_copy(part, part, b_send.at[v, h]).wait()
-
             def narrow(c, q):
                 rows = pl.ds(pl.multiple_of(c * rows_c, rows_c), rows_c)
                 z = jnp.concatenate([z_f32[j, rows, :] for j in range(pair_heads)], axis=1)
-                t_out[v, h, pl.ds(c * f_chunk, f_chunk)] = z.reshape(f_chunk, sub, width).astype(BF16)
+                z = z.reshape(f_chunk, sub, width).astype(BF16)
+
+                @pl.when(pair < pairs - 1)
+                def _():
+                    t_out[pair, v, h, pl.ds(c * f_chunk, f_chunk)] = z
+
+                @pl.when(pair == pairs - 1)
+                def _():
+                    y_ref[v, pl.ds(c * f_chunk, f_chunk), h] = z
                 return q
 
             lax.fori_loop(0, chunks, narrow, 0)
@@ -332,25 +330,28 @@
             @pl.when(pair < pairs - 1)
             def _():
                 def part(to):
-                    return t_out.at[v, h, pl.ds(to * f_loc, f_loc)], s_in.at[pair + 1, v, :, me * halves + h]
+                    return t_out.at[pair, v, h, pl.ds(to * f_loc, f_loc)], s_in.at[pair + 1, v, :, me * halves + h]
 
                 def send(to):
                     src, dst = part(to)
-                    pltpu.make_async_remote_copy(src_ref=src, dst_ref=dst, send_sem=b_send.at[v, h], recv_sem=b_recv.at[v], device_id={"sp": to}).start()
+                    pltpu.make_async_remote_copy(src_ref=src, dst_ref=dst, send_sem=b_send.at[pair, v, h], recv_sem=b_recv.at[pair, v], device_id={"sp": to}).start()
 
                 src, dst = part(me)
-                pltpu.make_async_copy(src, dst, b_recv.at[v]).start()
+                pltpu.make_async_copy(src, dst, b_recv.at[pair, v]).start()
                 spread(send)
-
-            @pl.when(pair == pairs - 1)
-            def _():
-                pltpu.make_async_copy(t_out.at[v, h], y_ref.at[v, :, h], y_sem.at[v, h]).start()
 
         lax.fori_loop(0, videos * halves, unit, 0)
 
     def run_pair(pair, carry):
         layer = 2 * pair
         wait_weights(layer, (0,))
+
+        @pl.when(pair == 0)
+        def _():
+            start_weights(0, 1)
+            for v in range(1, videos):
+                pltpu.make_async_copy(x_ref.at[v], s_in.at[0, v], x_sem.at[v]).start()
+
         spatial(pair)
         wait_weights(layer + 1, range(len(weights)))
 
@@ -365,10 +366,10 @@
 
     for v in range(videos):
         for h in range(halves):
-            done = y_ref.at[v, :, h]
-            pltpu.make_async_copy(done, done, y_sem.at[v, h]).wait()
+            part = t_in.at[0, v, h, pl.ds(0, frames - f_loc)]
+            for pair in range(pairs - 1):
+                pltpu.make_async_copy(part, part, b_send.at[pair, v, h]).wait()
             for pair in range(pairs):
-                part = t_in.at[pair, v, h, pl.ds(0, frames - f_loc)]
                 pltpu.make_async_copy(part, part, ac_send.at[pair, v, h if v else 0]).wait()
 
 
@@ -399,7 +400,7 @@
                 pltpu.VMEM((pairs, videos, f_loc, patches // SUB, SUB, width), BF16),
                 pltpu.VMEM((pairs, videos, f_loc, patches // SUB, SUB, width), BF16),
                 pltpu.VMEM((pairs, videos, halves, frames, SUB, width), BF16),
-                pltpu.VMEM((videos, halves, frames, SUB, width), BF16),
+                pltpu.VMEM((pairs - 1, videos, halves, frames, SUB, width), BF16),
                 pltpu.VMEM((width // head, LANES, patches), BF16),
                 pltpu.VMEM((patches, width), BF16),
                 pltpu.VMEM((width, patches), BF16),
@@ -415,11 +416,10 @@
                 pltpu.VMEM((4 * frames, 4 * frames), F32),
                 pltpu.SemaphoreType.DMA((layers, 4)),
                 pltpu.SemaphoreType.DMA((videos,)),
-                pltpu.SemaphoreType.DMA((videos,)),
+                pltpu.SemaphoreType.DMA((pairs - 1, videos)),
                 pltpu.SemaphoreType.DMA((pairs, videos, halves)),
-                pltpu.SemaphoreType.DMA((videos, halves)),
+                pltpu.SemaphoreType.DMA((pairs - 1, videos, halves)),
                 pltpu.SemaphoreType.DMA((pairs, videos, halves)),
-                pltpu.SemaphoreType.DMA((videos, halves)),
             ],
             compiler_params=pltpu.CompilerParams(collective_id=0, has_side_effects=True, vmem_limit_bytes=VMEM_BYTES),
             name="stack",

time: 101 us -> 99.1 us (0.981)
  the two profiles are of different devices: /device:TPU:22 before, /device:TPU:28 now
where the time goes in v7:
time: 99.1 us; the launch traced here: 99 us
  Pallas kernels  97.9 us (99%)
  local copies, waits for them, and re-layouts  1.02 us (1%)
    pallas_call x1, Pallas kernels, local_stack(): pl.pallas_call(functools.partial(kernel, n, head), out_shape=pltpu.VMEM((...  97.9 us

profile of v7, /device:TPU:28, one launch (start us, length us, event | category | flops | bytes accessed | tf_op | source)
XLA Modules:
  0.0 99.0 jit_solution(17553997597528239596)
XLA Ops:
  0.0 97.9 %stack.1 = bf16[2,48,2,8,384]{4,3,2,1,0:T(8,128)(2,1)S(1)} custom-call(bf16[2,3,32,8,384]{4,3,2,1,0:T(8,128)(2,1)} %bitcast.8, f32[4,4,384]{2,1,0:T(4,128)} %norms.1, bf16[4,1152,384]{2,1,0:T(8,128)(2,1)} %bitcast.7, bf16[4,384,384]{2,1,0:T(8,128)(2,1)} %bitcast.9, bf16[4,384,1536]{2,1,0:T(8,128)(2,1)} %wup_hbm.1, bf16[4,1536,384]{2,1,0:T(8,128)(2,1)} %wdown_hbm.1), custom_call_target="tpu_custom_call" | custom-call | tf_op jit(solution)/shard_map/stack/pallas_call | solution.py:390
  97.9 1.0 %copy.8 = bf16[2,48,16,384]{3,2,1,0:T(8,128)(2,1)} copy(bf16[2,48,16,384]{3,2,1,0:T(8,128)(2,1)S(1)} %bitcast.6) | data formatting | bytes 2359296

commit v8 on v7

--- a/solution.py
+++ b/solution.py
@@ -12,6 +12,7 @@
 SUB = 8
 VMEM_BYTES = 65_700_000
 ATTENTION_STEPS, MLP_STEPS = 12, 7
+UNIT_ORDER = "aaaaa" "abababababa" "bb" "a" "bbb" "cbcc" "b" "cccc" "ddddddd"
 GELU_A, GELU_B = math.sqrt(2 / math.pi), 0.044715
 F32, BF16 = jnp.float32, jnp.bfloat16
 
@@ -91,21 +92,21 @@
             out.append((lo, hi, lo // frames * frames, -(-hi // frames) * frames) if masked else (lo, hi, 0, rows))
         return out if masked else [(0, rows, 0, rows)]
 
-    def scores(h, rows, masked):
-        s = dot(k_s[pl.ds(0, rows), pl.ds(h * head // LANES * LANES, LANES)], q_s[h, :, pl.ds(0, rows)])
+    def scores(par, h, rows, masked):
+        s = dot(k_s[par, pl.ds(0, rows), pl.ds(h * head // LANES * LANES, LANES)], q_s[par, h, :, pl.ds(0, rows)])
         tops = []
         for lo, hi, k0, k1 in strips(rows, masked):
             part = s[k0:k1, lo:hi]
             if masked:
                 part = part + mask_s[pl.ds(k0, k1 - k0), pl.ds(lo, hi - lo)]
-            s_s[h, pl.ds(k0, k1 - k0), pl.ds(lo, hi - lo)] = part
+            s_s[par, h, pl.ds(k0, k1 - k0), pl.ds(lo, hi - lo)] = part
             tops.append(jnp.max(part, axis=0, keepdims=True) + math.log(rows))
         return tops
 
-    def mix(h, rows, masked, tops):
+    def mix(par, h, rows, masked, tops):
         cols, sums = [], []
         for (lo, hi, k0, k1), top in zip(strips(rows, masked), tops):
-            e = jnp.exp(s_s[h, pl.ds(k0, k1 - k0), pl.ds(lo, hi - lo)] - top)
+            e = jnp.exp(s_s[par, h, pl.ds(k0, k1 - k0), pl.ds(lo, hi - lo)] - top)
             sums.append(jnp.sum(e, axis=0, keepdims=True))
             col = [jnp.zeros((k, hi - lo), BF16) for k in (k0,)] if k0 else []
             col.append(e.astype(BF16))
@@ -114,47 +115,51 @@
             cols.append(jnp.concatenate(col, axis=0) if len(col) > 1 else col[0])
         p = jnp.concatenate(cols, axis=1) if len(cols) > 1 else cols[0]
         norm = jnp.concatenate(sums, axis=1) if len(sums) > 1 else sums[0]
-        o = dot(v_s[pl.ds(h * head, head), pl.ds(0, rows)], p)
-        ot_s[pl.ds(h * head, head), pl.ds(0, rows)] = (o * (1.0 / norm)).astype(BF16)
+        o = dot(v_s[par, pl.ds(h * head, head), pl.ds(0, rows)], p)
+        ot_s[par, pl.ds(h * head, head), pl.ds(0, rows)] = (o * (1.0 / norm)).astype(BF16)
 
     def gelu(x):
         t = jnp.tanh(x * (GELU_A + (GELU_A * GELU_B) * (x * x)))
         half = 0.5 * x
         return half + half * t
 
-    def attention_steps(get, rows, layer, masked):
+    def attention_steps(get, rows, layer, masked, par=0):
         a = layer_norm(get(), norms[layer, pl.ds(0, 1), :], norms[layer, pl.ds(1, 1), :]).astype(BF16)
         yield
         q = (dot_nt(wqkv[layer, pl.ds(0, width), :], a) * scale).astype(BF16)
         for h in range(heads):
-            q_s[h, pl.ds(h * head % LANES, head), pl.ds(0, rows)] = q[h * head:(h + 1) * head]
-        yield
-        k_s[pl.ds(0, rows), :] = dot_nt(a, wqkv[layer, pl.ds(width, width), :]).astype(BF16)
-        yield
-        v_s[:, pl.ds(0, rows)] = dot_nt(wqkv[layer, pl.ds(2 * width, width), :], a).astype(BF16)
+            q_s[par, h, pl.ds(h * head % LANES, head), pl.ds(0, rows)] = q[h * head:(h + 1) * head]
+        yield
+        k_s[par, pl.ds(0, rows), :] = dot_nt(a, wqkv[layer, pl.ds(width, width), :]).astype(BF16)
+        yield
+        v_s[par, :, pl.ds(0, rows)] = dot_nt(wqkv[layer, pl.ds(2 * width, width), :], a).astype(BF16)
         yield
         ahead = 2
-        tops = [scores(h, rows, masked) for h in range(ahead)]
+        tops = [scores(par, h, rows, masked) for h in range(ahead)]
         yield
         for h in range(heads):
             if h + ahead < heads:
-                tops.append(scores(h + ahead, rows, masked))
-            mix(h, rows, masked, tops[h])
+                tops.append(scores(par, h + ahead, rows, masked))
+            mix(par, h, rows, masked, tops[h])
             yield
-        h = (get() + dot_tn(ot_s[:, pl.ds(0, rows)], wout[layer])).astype(BF16)
-        next_h[pl.ds(0, rows), :] = h
-        next_a[pl.ds(0, rows), :] = layer_norm(h.astype(F32), norms[layer, pl.ds(2, 1), :], norms[layer, pl.ds(3, 1), :]).astype(BF16)
-        yield
-
-    def mlp_steps(rows, layer, put):
-        cur_h[pl.ds(0, rows), :] = next_h[pl.ds(0, rows), :]
-        cur_a[pl.ds(0, rows), :] = next_a[pl.ds(0, rows), :]
+        h = (get() + dot_tn(ot_s[par, :, pl.ds(0, rows)], wout[layer])).astype(BF16)
+        next_h[par, pl.ds(0, rows), :] = h
+        next_a[par, pl.ds(0, rows), :] = layer_norm(h.astype(F32), norms[layer, pl.ds(2, 1), :], norms[layer, pl.ds(3, 1), :]).astype(BF16)
+        yield
+
+    def mlp_steps(rows, layer, put, par=None):
+        if par is None:
+            cur_h[pl.ds(0, rows), :] = next_h[0, pl.ds(0, rows), :]
+            cur_a[pl.ds(0, rows), :] = next_a[0, pl.ds(0, rows), :]
+            h_ref, a_ref, par = cur_h, cur_a, 0
+        else:
+            h_ref, a_ref = next_h.at[par], next_a.at[par]
         chunk = 256
-        for c in range(hid_s.shape[1] // chunk):
-            up = dot(cur_a[pl.ds(0, rows), :], wup[layer, :, pl.ds(c * chunk, chunk)])
-            hid_s[pl.ds(0, rows), pl.ds(c * chunk, chunk)] = gelu(up).astype(BF16)
+        for c in range(hid_s.shape[2] // chunk):
+            up = dot(a_ref[pl.ds(0, rows), :], wup[layer, :, pl.ds(c * chunk, chunk)])
+            hid_s[par, pl.ds(0, rows), pl.ds(c * chunk, chunk)] = gelu(up).astype(BF16)
             yield
-        put(cur_h[pl.ds(0, rows), :].astype(F32) + dot(hid_s[pl.ds(0, rows), :], wdown[layer]))
+        put(h_ref[pl.ds(0, rows), :].astype(F32) + dot(hid_s[par, pl.ds(0, rows), :], wdown[layer]))
         yield
 
     def emit(first, second):
@@ -291,7 +296,9 @@
                 return q
 
             lax.fori_loop(0, chunks, widen, 0)
-            pipeline(groups, attention, mlp, lambda g: None)
+            streams = {"a": attention(0), "b": attention(1), "c": mlp(0), "d": mlp(1)}
+            for step in UNIT_ORDER:
+                next(streams[step])
             finish(v, h)
             return carry
 
@@ -300,7 +307,7 @@
                 return jnp.concatenate([jnp.concatenate([u_f32[j, pl.ds(g * group + p, frames, stride=sub), :] for p in range(group)], axis=0)
                                         for j in range(pair_heads)], axis=1)
 
-            return attention_steps(get, rows_g, layer, True)
+            return attention_steps(get, rows_g, layer, True, g)
 
         def mlp(g):
             def put(z):
@@ -308,7 +315,7 @@
                     for j in range(pair_heads):
                         z_f32[j, pl.ds(g * group + p, frames, stride=sub), :] = z[p * frames:(p + 1) * frames, j * LANES:(j + 1) * LANES]
 
-            return mlp_steps(rows_g, layer, put)
+            return mlp_steps(rows_g, layer, put, g)
 
         def finish(v, h):
             def narrow(c, q):
@@ -401,14 +408,14 @@
                 pltpu.VMEM((pairs, videos, f_loc, patches // SUB, SUB, width), BF16),
                 pltpu.VMEM((pairs, videos, halves, frames, SUB, width), BF16),
                 pltpu.VMEM((pairs - 1, videos, halves, frames, SUB, width), BF16),
-                pltpu.VMEM((width // head, LANES, patches), BF16),
-                pltpu.VMEM((patches, width), BF16),
-                pltpu.VMEM((width, patches), BF16),
-                pltpu.VMEM((width, patches), BF16),
-                pltpu.VMEM((width // head, patches, patches), F32),
-                pltpu.VMEM((patches, hidden), BF16),
-                pltpu.VMEM((patches, width), BF16),
-                pltpu.VMEM((patches, width), BF16),
+                pltpu.VMEM((2, width // head, LANES, patches), BF16),
+                pltpu.VMEM((2, patches, width), BF16),
+                pltpu.VMEM((2, width, patches), BF16),
+                pltpu.VMEM((2, width, patches), BF16),
+                pltpu.VMEM((2, width // head, patches, patches), F32),
+                pltpu.VMEM((2, patches, hidden), BF16),
+                pltpu.VMEM((2, patches, width), BF16),
+                pltpu.VMEM((2, patches, width), BF16),
                 pltpu.VMEM((patches, width), BF16),
                 pltpu.VMEM((patches, width), BF16),
                 pltpu.VMEM((width // LANES, frames * SUB, LANES), F32),

time: 99.1 us -> 97.1 us (0.980)
  the two profiles are of different devices: /device:TPU:28 before, /device:TPU:21 now
where the time goes in v8:
time: 97.1 us; the launch traced here: 96 us
  Pallas kernels  95 us (98%)
  local copies, waits for them, and re-layouts  1.02 us (1%)
    pallas_call x1, Pallas kernels, local_stack(): pl.pallas_call(functools.partial(kernel, n, head), out_shape=pltpu.VMEM((...  95 us

profile of v8, /device:TPU:21, one launch (start us, length us, event | category | flops | bytes accessed | tf_op | source)
XLA Modules:
  0.0 96.0 jit_solution(3441869643984649985)
XLA Ops:
  0.0 95.0 %stack.1 = bf16[2,48,2,8,384]{4,3,2,1,0:T(8,128)(2,1)S(1)} custom-call(bf16[2,3,32,8,384]{4,3,2,1,0:T(8,128)(2,1)} %bitcast.8, f32[4,4,384]{2,1,0:T(4,128)} %norms.1, bf16[4,1152,384]{2,1,0:T(8,128)(2,1)} %bitcast.7, bf16[4,384,384]{2,1,0:T(8,128)(2,1)} %bitcast.9, bf16[4,384,1536]{2,1,0:T(8,128)(2,1)} %wup_hbm.1, bf16[4,1536,384]{2,1,0:T(8,128)(2,1)} %wdown_hbm.1), custom_call_target="tpu_custom_call" | custom-call | tf_op jit(solution)/shard_map/stack/pallas_call | solution.py:397
  95.0 1.0 %copy.8 = bf16[2,48,16,384]{3,2,1,0:T(8,128)(2,1)} copy(bf16[2,48,16,384]{3,2,1,0:T(8,128)(2,1)S(1)} %bitcast.6) | data formatting | bytes 2359296

commit v9 on v8

--- a/solution.py
+++ b/solution.py
@@ -147,7 +147,7 @@
         next_a[par, pl.ds(0, rows), :] = layer_norm(h.astype(F32), norms[layer, pl.ds(2, 1), :], norms[layer, pl.ds(3, 1), :]).astype(BF16)
         yield
 
-    def mlp_steps(rows, layer, put, par=None):
+    def mlp_steps(rows, layer, put, par=None, row0=0):
         if par is None:
             cur_h[pl.ds(0, rows), :] = next_h[0, pl.ds(0, rows), :]
             cur_a[pl.ds(0, rows), :] = next_a[0, pl.ds(0, rows), :]
@@ -156,10 +156,10 @@
             h_ref, a_ref = next_h.at[par], next_a.at[par]
         chunk = 256
         for c in range(hid_s.shape[2] // chunk):
-            up = dot(a_ref[pl.ds(0, rows), :], wup[layer, :, pl.ds(c * chunk, chunk)])
+            up = dot(a_ref[pl.ds(row0, rows), :], wup[layer, :, pl.ds(c * chunk, chunk)])
             hid_s[par, pl.ds(0, rows), pl.ds(c * chunk, chunk)] = gelu(up).astype(BF16)
             yield
-        put(h_ref[pl.ds(0, rows), :].astype(F32) + dot(hid_s[par, pl.ds(0, rows), :], wdown[layer]))
+        put(h_ref[pl.ds(row0, rows), :].astype(F32) + dot(hid_s[par, pl.ds(0, rows), :], wdown[layer]))
         yield
 
     def emit(first, second):
@@ -169,22 +169,19 @@
             if stage is not None:
                 next(stage)
 
-    def pipeline(tiles_n, attention, mlp, after, alone=None, late=None):
+    def pipeline(tiles_n, attention, mlp, after, alone, first, late):
         steps = attention(0)
         for _ in range(ATTENTION_STEPS - 1):
             next(steps)
-        if late is not None:
-            late()
+        late()
         next(steps)
-        start = 1
-        if alone is not None:
-            @pl.when(alone)
-            def _():
-                emit(None, mlp(0))
-                after(0)
-                emit(attention(1), None)
-
-            start = jnp.where(alone, 2, 1)
+
+        @pl.when(alone)
+        def _():
+            first()
+            emit(attention(1), None)
+
+        start = jnp.where(alone, 2, 1)
 
         def step(i, c):
             emit(attention(i), mlp(i - 1))
@@ -247,10 +244,6 @@
                 return mlp_steps(patches, layer, put)
 
             def after(f):
-                @pl.when((pair == 0) & (v == 0) & (f == 0))
-                def _():
-                    pl.semaphore_wait(barrier, n - 1)
-
                 @pl.when(v == 0)
                 def _():
                     send_frame(pair, v, f)
@@ -266,7 +259,36 @@
                     wait_weights(layer, (1, 2, 3))
                     start_weights(layer + 1)
 
-            pipeline(f_loc, attention, mlp, after, (pair == 0) & (v == 0), late)
+            def first():
+                rows, cut = patches // 2, tiles // 2
+
+                def part(to):
+                    return s_out.at[pair, v, 0, pl.ds(to * halves, halves)], t_in.at[pair, v, :, me * f_loc]
+
+                def rows_of(r, q):
+                    def put(z):
+                        s_out[pair, v, 0, pl.ds(r * cut, cut)] = z.reshape(cut, sub, width).astype(BF16)
+
+                    emit(None, mlp_steps(rows, layer, put, 0, pl.multiple_of(r * rows, rows)))
+
+                    @pl.when(r == 0)
+                    def _():
+                        pl.semaphore_wait(barrier, n - 1)
+
+                    for i in range(n // 2):
+                        to = r * (n // 2) + lax.rem(me + n // 4 + i, n // 2)
+
+                        @pl.when(to != me)
+                        def _():
+                            src, dst = part(to)
+                            pltpu.make_async_remote_copy(src_ref=src, dst_ref=dst, send_sem=ac_send.at[pair, v, 0], recv_sem=ac_recv.at[pair, v, 0], device_id={"sp": to}).start()
+                    return q
+
+                lax.fori_loop(0, 2, rows_of, 0)
+                src, dst = part(me)
+                pltpu.make_async_copy(src, dst, ac_recv.at[pair, v, 0]).start()
+
+            pipeline(f_loc, attention, mlp, after, (pair == 0) & (v == 0), first, late)
             return c
 
         lax.fori_loop(0, videos, video, 0)

time: 97.1 us -> 98 us (level)
  Pallas kernels: 95 us -> 96.5 us
    pallas_call x1, Pallas kernels: 95 us -> 96.5 us  [local_stack(): pl.pallas_call(functools.partial(kernel, n, head), out_shape=pltpu.VMEM((...]
where the time goes in v9:
time: 98 us; the launch traced here: 97.5 us
  Pallas kernels  96.5 us (98%)
  local copies, waits for them, and re-layouts  1.02 us (1%)
    pallas_call x1, Pallas kernels, local_stack(): pl.pallas_call(functools.partial(kernel, n, head), out_shape=pltpu.VMEM((...  96.5 us

profile of v9, /device:TPU:21, one launch (start us, length us, event | category | flops | bytes accessed | tf_op | source)
XLA Modules:
  0.0 97.5 jit_solution(11760351900282666878)
XLA Ops:
  0.0 96.5 %stack.1 = bf16[2,48,2,8,384]{4,3,2,1,0:T(8,128)(2,1)S(1)} custom-call(bf16[2,3,32,8,384]{4,3,2,1,0:T(8,128)(2,1)} %bitcast.8, f32[4,4,384]{2,1,0:T(4,128)} %norms.1, bf16[4,1152,384]{2,1,0:T(8,128)(2,1)} %bitcast.7, bf16[4,384,384]{2,1,0:T(8,128)(2,1)} %bitcast.9, bf16[4,384,1536]{2,1,0:T(8,128)(2,1)} %wup_hbm.1, bf16[4,1536,384]{2,1,0:T(8,128)(2,1)} %wdown_hbm.1), custom_call_target="tpu_custom_call" | custom-call | tf_op jit(solution)/shard_map/stack/pallas_call | solution.py:419
  96.5 1.0 %copy.8 = bf16[2,48,16,384]{3,2,1,0:T(8,128)(2,1)} copy(bf16[2,48,16,384]{3,2,1,0:T(8,128)(2,1)S(1)} %bitcast.6) | data formatting | bytes 2359296
